TPU v7x, 32 devices: a whole 2x2x4 slice. The times are simulated.
32 devices in a mesh: row: 4 (over z), col: 8 (over y, x, core).
Axes of the slice: x: 2, y: 2, z: 4, core: 2. Of those that a mesh axis runs over, the one named last changes fastest.
Arguments:
- tokens_in: bfloat16 [8192, 1408], P(('row', 'col')), may hold values from -300 to 300
- ln1_gain: bfloat16 [1408], replicated, may hold values from 0.099609375 to 1.8984375
- ln1_bias: bfloat16 [1408], replicated, may hold values from -3 to 3
- qkv_weight: bfloat16 [1408, 4224], P('row', 'col'), may hold values from -0.8 to 0.8
- qkv_bias: bfloat16 [4224], P('col'), may hold values from -3 to 3
- proj_weight: bfloat16 [1408, 1408], P('col', 'row'), may hold values from -0.15625 to 0.15625
- proj_bias: bfloat16 [1408], replicated, may hold values from -3 to 3
- ln2_gain: bfloat16 [1408], replicated, may hold values from 0.099609375 to 1.8984375
- ln2_bias: bfloat16 [1408], replicated, may hold values from -3 to 3
- fc1_weight: bfloat16 [1408, 6144], P('row', 'col'), may hold values from -0.15625 to 0.15625
- fc1_bias: bfloat16 [6144], P('col'), may hold values from -3 to 3
- fc2_weight: bfloat16 [1408, 6144], P('row', 'col'), may hold values from -0.078125 to 0.078125
- fc2_bias: bfloat16 [1408], replicated, may hold values from -3 to 3
Outputs:
- tokens_out: bfloat16 [8192, 1408], P(('row', 'col'))
All inputs are finite; a program needn't handle non-finite values.
Results may differ from a plain program's by a relative error of at most 0.01.
Values may be sent and summed in bfloat16 or wider, within the bound.
A program may use at most 64 MiB of HBM per device.

v0:
```python
import functools

import jax
import jax.numpy as jnp
from jax import lax
from jax.experimental import pallas as pl
from jax.experimental.pallas import tpu as pltpu
from jax.sharding import PartitionSpec as P

HEADS = 16
LANES = 128
MESH = pl.DeviceIdType.MESH


def greet(peers):
    barrier = pltpu.get_barrier_semaphore()
    for peer in peers:
        pl.semaphore_signal(barrier, inc=1, device_id={"col": peer}, device_id_type=MESH)
    pl.semaphore_wait(barrier, len(peers))


def neighbours():
    me = lax.axis_index("col")
    core, x, y = me % 2, (me // 2) % 2, me // 4
    place = lambda y, x, core: y * 4 + x * 2 + core
    return (
        me,
        place(y, x, 1 - core),
        place(y, 1 - x, core),
        place(1 - y, x, core),
        place(1 - y, 1 - x, core),
    )


def gather_kernel(x_ref, o_ref, send, recv, local_sem):
    rows = x_ref.shape[0]
    half = rows // 2
    me, mate, xn, yn, dn = neighbours()
    greet((mate, xn, yn))

    def part(block, h):
        return o_ref.at[pl.ds(pl.multiple_of(block * rows + h * half, half), half)]

    def copy(i, src, block, h, to):
        return pltpu.make_async_remote_copy(
            src_ref=src, dst_ref=part(block, h), send_sem=send.at[i], recv_sem=recv.at[i],
            device_id={"col": to}, device_id_type=MESH,
        )

    def own(h):
        return x_ref.at[pl.ds(h * half, half)]

    def arrived(i, block, h):
        copy(i, own(0), block, h, mate).wait_recv()

    started = []

    def go(c):
        c.start()
        started.append(c)

    go(copy(0, own(0), me, 0, xn))
    go(copy(1, own(1), me, 1, yn))
    go(copy(2, own(1), me, 1, xn))
    go(copy(3, own(0), me, 0, yn))
    go(copy(6, own(0), me, 0, mate))
    go(copy(7, own(1), me, 1, mate))
    here = pltpu.make_async_copy(
        x_ref, o_ref.at[pl.ds(pl.multiple_of(me * rows, rows), rows)], local_sem
    )
    here.start()
    arrived(0, xn, 0)
    go(copy(4, part(xn, 0), xn, 0, yn))
    go(copy(8, part(xn, 0), xn, 0, mate))
    arrived(1, yn, 1)
    go(copy(5, part(yn, 1), yn, 1, xn))
    go(copy(9, part(yn, 1), yn, 1, mate))
    arrived(2, xn, 1)
    go(copy(10, part(xn, 1), xn, 1, mate))
    arrived(3, yn, 0)
    go(copy(11, part(yn, 0), yn, 0, mate))
    arrived(4, dn, 0)
    go(copy(12, part(dn, 0), dn, 0, mate))
    arrived(5, dn, 1)
    go(copy(13, part(dn, 1), dn, 1, mate))
    across = lambda block: block + mate - me
    for i, block, h in (
        (6, me, 0), (7, me, 1), (8, xn, 0), (9, yn, 1),
        (10, xn, 1), (11, yn, 0), (12, dn, 0), (13, dn, 1),
    ):
        arrived(i, across(block), h)
    for c in started:
        c.wait_send()
    here.wait()


def gather_col(x, collective_id):
    n = lax.axis_size("col")
    rows, width = x.shape
    if n != 8 or rows % 32:
        return lax.all_gather(x, "col", axis=0, tiled=True)
    return pl.pallas_call(
        gather_kernel,
        out_shape=jax.ShapeDtypeStruct((n * rows, width), x.dtype),
        in_specs=[pl.BlockSpec(memory_space=pltpu.VMEM)],
        out_specs=pl.BlockSpec(memory_space=pltpu.VMEM),
        scratch_shapes=[
            pltpu.SemaphoreType.DMA((14,)),
            pltpu.SemaphoreType.DMA((14,)),
            pltpu.SemaphoreType.DMA,
        ],
        compiler_params=pltpu.CompilerParams(
            collective_id=collective_id, has_side_effects=True, vmem_limit_bytes=24 << 20
        ),
        cost_estimate=pl.CostEstimate(
            flops=10**10, bytes_accessed=2 * n * rows * width, transcendentals=0
        ),
        name="gather_col",
    )(x)


def scatter_kernel(x_ref, o_ref, mated, sums, relay, landed, send, recv):
    rows = o_ref.shape[0]
    half = rows // 2
    me, mate, xn, yn, dn = neighbours()
    greet((mate, xn, yn))
    shift = mate - me
    targets = (dn, xn, yn, me)

    def copy(i, src, dst, to):
        return pltpu.make_async_remote_copy(
            src_ref=src, dst_ref=dst, send_sem=send.at[i], recv_sem=recv.at[i],
            device_id={"col": to}, device_id_type=MESH,
        )

    def block(j):
        return pl.ds(pl.multiple_of(j * rows, rows), rows)

    started = []

    def go(c):
        c.start()
        started.append(c)

    for k, target in enumerate(targets):
        go(copy(k, x_ref.at[block(target + shift)], mated.at[k], mate))

    def mine(k, h):
        rows_h = pl.ds(pl.multiple_of(targets[k] * rows + h * half, half), half)
        return x_ref[rows_h, :].astype(jnp.float32) + mated[k, pl.ds(h * half, half), :].astype(
            jnp.float32
        )

    def put(k, h, value):
        sums[k, pl.ds(h * half, half), :] = value.astype(jnp.bfloat16)

    def of(ref, k, h):
        return ref.at[k, pl.ds(h * half, half)]

    started[0].wait_recv()
    put(0, 0, mine(0, 0))
    go(copy(4, of(sums, 0, 0), relay.at[0], xn))
    put(0, 1, mine(0, 1))
    go(copy(5, of(sums, 0, 1), relay.at[1], yn))
    started[1].wait_recv()
    put(1, 0, mine(1, 0))
    go(copy(6, of(sums, 1, 0), of(landed, 0, 0), xn))
    started[2].wait_recv()
    put(2, 1, mine(2, 1))
    go(copy(7, of(sums, 2, 1), of(landed, 1, 1), yn))
    started[4].wait_recv()
    put(2, 0, mine(2, 0) + relay[0].astype(jnp.float32))
    go(copy(8, of(sums, 2, 0), of(landed, 1, 0), yn))
    started[5].wait_recv()
    put(1, 1, mine(1, 1) + relay[1].astype(jnp.float32))
    go(copy(9, of(sums, 1, 1), of(landed, 0, 1), xn))
    started[3].wait_recv()
    for i in (6, 7, 8, 9):
        started[i].wait_recv()
    for h in (0, 1):
        lines = pl.ds(h * half, half)
        o_ref[lines, :] = (
            mine(3, h)
            + landed[0, lines, :].astype(jnp.float32)
            + landed[1, lines, :].astype(jnp.float32)
        )
    for c in started:
        c.wait_send()


def scatter_col(x, collective_id):
    n = lax.axis_size("col")
    rows, width = x.shape[0] // n, x.shape[1]
    if n != 8 or rows % 32:
        return lax.psum_scatter(x, "col", scatter_dimension=0, tiled=True).astype(jnp.float32)
    return pl.pallas_call(
        scatter_kernel,
        out_shape=jax.ShapeDtypeStruct((rows, width), jnp.float32),
        in_specs=[pl.BlockSpec(memory_space=pltpu.VMEM)],
        out_specs=pl.BlockSpec(memory_space=pltpu.VMEM),
        scratch_shapes=[
            pltpu.VMEM((4, rows, width), x.dtype),
            pltpu.VMEM((3, rows, width), x.dtype),
            pltpu.VMEM((2, rows // 2, width), x.dtype),
            pltpu.VMEM((2, rows, width), x.dtype),
            pltpu.SemaphoreType.DMA((10,)),
            pltpu.SemaphoreType.DMA((10,)),
        ],
        compiler_params=pltpu.CompilerParams(
            collective_id=collective_id, has_side_effects=True, vmem_limit_bytes=32 << 20
        ),
        cost_estimate=pl.CostEstimate(
            flops=10**10, bytes_accessed=2 * n * rows * width, transcendentals=0
        ),
        name="scatter_col",
    )(x)


def gather_row(weight, axis):
    n = lax.axis_size("row")
    me = lax.axis_index("row")
    depth = weight.shape[axis]
    shape = list(weight.shape)
    shape[axis] *= n
    whole = jnp.zeros(shape, weight.dtype)
    for step in range(n):
        block = weight
        if step:
            block = lax.ppermute(weight, "row", [((i + step) % n, i) for i in range(n)])
        whole = lax.dynamic_update_slice_in_dim(whole, block, ((me + step) % n) * depth, axis)
    return whole


def cube_gather_col(x):
    n = lax.axis_size("col")
    if n != 8:
        return lax.all_gather(x, "col", axis=0, tiled=True)
    me = lax.axis_index("col")
    x = x[None]
    for bit, after in ((2, 1), (4, 2), (1, 4)):
        other = lax.ppermute(x, "col", [(i, i ^ bit) for i in range(n)])
        low = (me // bit) % 2 == 0
        first, second = jnp.where(low, x, other), jnp.where(low, other, x)
        x = jnp.concatenate([first, second], axis=0) if bit != 1 else jnp.stack([first, second], 1)
    return x.reshape(-1, x.shape[-1])


def norm_local(values, gain, bias):
    mean = jnp.mean(values, axis=-1, keepdims=True)
    centred = values - mean
    var = jnp.mean(centred * centred, axis=-1, keepdims=True)
    return centred * lax.rsqrt(var + 1e-06) * gain.astype(jnp.float32) + bias.astype(jnp.float32)


def attend_kernel(heads, size, padded, q_ref, kv_ref, o_ref):
    outs = []
    for head in range(heads):
        base = head * 3 * padded
        query = q_ref[:, base : base + padded]
        keys = kv_ref[:, base + padded : base + 2 * padded]
        values = kv_ref[:, base + 2 * padded : base + 3 * padded]
        scores = lax.dot_general(
            query, keys, (((1,), (1,)), ((), ())), preferred_element_type=jnp.float32
        )
        top = jnp.max(scores, axis=-1, keepdims=True)
        expo = jnp.exp2(scores - top).astype(jnp.bfloat16)
        mixed = jnp.dot(expo, values, preferred_element_type=jnp.float32)
        outs.append(mixed[:, :size] / mixed[:, size : size + 1])
    o_ref[...] = jnp.concatenate(outs, axis=1).astype(o_ref.dtype)


def attend(qkv, heads, size, padded):
    length, width = qkv.shape
    block = min(256, length)
    return pl.pallas_call(
        functools.partial(attend_kernel, heads, size, padded),
        grid=(length // block,),
        in_specs=[
            pl.BlockSpec((block, width), lambda i: (i, 0)),
            pl.BlockSpec((length, width), lambda i: (0, 0)),
        ],
        out_specs=pl.BlockSpec((block, heads * size), lambda i: (i, 0)),
        out_shape=jax.ShapeDtypeStruct((length, heads * size), jnp.bfloat16),
        compiler_params=pltpu.CompilerParams(vmem_limit_bytes=40 << 20),
        cost_estimate=pl.CostEstimate(
            flops=4 * heads * length * length * padded * 8,
            bytes_accessed=4 * length * width,
            transcendentals=heads * length * length,
        ),
        name="attend",
    )(qkv, qkv)


def project_back(left, right):
    return lax.dot_general(
        left, right, (((1,), (1,)), ((), ())), preferred_element_type=jnp.float32
    )


def fast_plan(heads, own_rows, features, qkv_width, proj_rows, hidden):
    if lax.axis_size("col") != 8 or lax.axis_size("row") != 4:
        return None
    quarter = features // 4
    size = qkv_width // (3 * heads)
    whole = qkv_width // LANES * LANES
    rest = qkv_width - whole
    ok = (
        own_rows % 32 == 0 and features % LANES == 0 and quarter % 32 == 0
        and hidden % LANES == 0 and 0 < rest and proj_rows == heads * size
        and proj_rows % 16 == 0 and size < LANES and whole // size == 3 * heads - 1
    )
    if not ok:
        return None
    first = 2 * quarter // LANES * LANES
    last = -(-quarter // LANES) * LANES
    middle = features - first - last
    if middle <= 0 or features - last > 3 * quarter:
        return None
    return dict(
        heads=heads, size=size, rows=own_rows, features=features, quarter=quarter, whole=whole,
        rest=rest, proj_rows=proj_rows, slot=-(-proj_rows // LANES) * LANES, hidden=hidden,
        pieces=(first, middle, last),
    )


def layer_kernel(
    plan, tok, vec, wq, wp, w1, w2, o_ref,
    x1, x2, qmain, qrest, qwide, qrow, qkv, ctx, ctx_out, pfull, f1, f2, resid, hid, part,
    mated, sums, relay, landed,
    zsend, zrecv, gsend, grecv, psend, precv, asend, arecv, ssend, srecv,
):
    heads, size, rows = plan["heads"], plan["size"], plan["rows"]
    features, quarter = plan["features"], plan["quarter"]
    whole, rest, slot, prows = plan["whole"], plan["rest"], plan["slot"], plan["proj_rows"]
    hidden, pieces = plan["hidden"], plan["pieces"]
    half = rows // 2
    groups = 3 * heads
    f32, bf16 = jnp.float32, jnp.bfloat16

    row = lax.axis_index("row")
    me, mate, xn, yn, dn = neighbours()
    shift = mate - me
    pair = row // 2
    near = row + 1 - 2 * (row % 2)
    other = 2 - pair
    far = 3 - 3 * pair
    middle = jnp.logical_or(row == 1, row == 2)
    end = jnp.logical_or(row == 0, row == 3)
    lo = 2 * pair
    hi = 2 - lo

    def flipped(mask):
        bits = [(me % 2 + mask % 2) % 2, (me // 2 % 2 + mask // 2 % 2) % 2, (me // 4 + mask // 4) % 2]
        return bits[0] + 2 * bits[1] + 4 * bits[2]

    barrier = pltpu.get_barrier_semaphore()
    for step in range(1, 8):
        pl.semaphore_signal(
            barrier, inc=1, device_id={"col": flipped(step)}, device_id_type=MESH
        )
    for step in range(1, 4):
        pl.semaphore_signal(
            barrier, inc=1, device_id={"row": (row + step) % 4}, device_id_type=MESH
        )

    def remote(src, dst, ssem, rsem, **to):
        return pltpu.make_async_remote_copy(
            src_ref=src, dst_ref=dst, send_sem=ssem, recv_sem=rsem,
            device_id=to, device_id_type=MESH,
        )

    def lines(b, n=rows):
        return pl.ds(pl.multiple_of(b * n, n), n)

    def place(w, b):
        if w == 0:
            return qmain.at[lines(b, quarter)]
        if w == 1:
            return qrest.at[b]
        if w == 2:
            return pfull.at[b, lines(me, slot)].at[pl.ds(0, prows)]
        return (f1 if w == 3 else f2).at[lines(b, quarter)]

    def source(w):
        if w == 0:
            return wq.at[:, pl.ds(0, whole)]
        return (None, qrest.at[row], wp, w1, w2)[w]

    def own_copy(w, s):
        return remote(
            source(w), place(w, row), zsend.at[w * 4 + s], zrecv.at[w * 4 + row],
            row=near if s == 0 else other,
        )

    def forward_copy(w, s, b):
        return remote(
            place(w, b), place(w, b), zsend.at[w * 4 + s], zrecv.at[w * 4 + b], row=near
        )

    def z_wait(w, b):
        remote(
            place(w, b), place(w, b), zsend.at[w * 4], zrecv.at[w * 4 + b], row=near
        ).wait_recv()

    def z_forward(w, s, b):
        z_wait(w, b)
        forward_copy(w, s, b).start()

    for j in range(quarter // 32):
        qrest[row, :, j * rest : (j + 1) * rest] = wq[32 * j : 32 * (j + 1), whole:]
    pl.semaphore_wait(barrier, 10)
    for w in (0, 2):
        for s in (0, 1):
            own_copy(w, s).start()

    def norm(values, g, b):
        mean = jnp.mean(values, axis=-1, keepdims=True)
        centred = values - mean
        var = jnp.mean(centred * centred, axis=-1, keepdims=True)
        return centred * lax.rsqrt(var + 1e-06) * vec[g : g + 1, :] + vec[b : b + 1, :]

    chunk = 32

    def norm1(i, c):
        at = pl.ds(pl.multiple_of(i * chunk, chunk), chunk)
        to = pl.ds(pl.multiple_of(me * rows + i * chunk, chunk), chunk)
        x1[to, :] = norm(tok[at, :].astype(f32), 0, 1).astype(bf16)
        return c

    lax.fori_loop(0, rows // chunk, norm1, 0)
    for s in (0, 1):
        own_copy(1, s).start()

    class Gather:
        def __init__(self, x, gi):
            self.x, self.gi = x, gi

        def copy(self, i, block, h, to):
            at = self.x.at[pl.ds(pl.multiple_of(block * rows + h * half, half), half)]
            return remote(at, at, gsend.at[self.gi, i], grecv.at[self.gi, i], col=to)

        def arrived(self, i, block, h):
            self.copy(i, block, h, mate).wait_recv()

        def start(self):
            for i, h, to in ((0, 0, xn), (1, 1, yn), (2, 1, xn), (3, 0, yn), (6, 0, mate), (7, 1, mate)):
                self.copy(i, me, h, to).start()

        def event0(self):
            self.arrived(0, xn, 0)
            self.copy(4, xn, 0, yn).start()
            self.copy(8, xn, 0, mate).start()
            self.arrived(1, yn, 1)
            self.copy(5, yn, 1, xn).start()
            self.copy(9, yn, 1, mate).start()

        def event1(self):
            self.arrived(2, xn, 1)
            self.copy(10, xn, 1, mate).start()
            self.arrived(3, yn, 0)
            self.copy(11, yn, 0, mate).start()

        def event2(self):
            self.arrived(4, dn, 0)
            self.copy(12, dn, 0, mate).start()
            self.arrived(5, dn, 1)
            self.copy(13, dn, 1, mate).start()

        def mate0(self):
            self.arrived(6, mate, 0)
            self.arrived(7, mate, 1)

        def mate1(self):
            for i, block, h in ((8, xn, 0), (10, xn, 1), (9, yn, 1), (11, yn, 0)):
                self.arrived(i, block + shift, h)

        def mate2(self):
            for i, h in ((12, 0), (13, 1)):
                self.arrived(i, dn + shift, h)

        def finish(self):
            for i in range(14):
                self.copy(i, me, 0, mate).wait_send()

    first = Gather(x1, 0)
    first.start()
    for w in (3, 4):
        @pl.when(end)
        def _():
            own_copy(w, 0).start()

        own_copy(w, 1).start()

    qrow[...] = jnp.zeros_like(qrow)
    for g in range(groups):
        qrow[:, g * LANES : g * LANES + size] = vec[6:7, g * size : (g + 1) * size]
    lane = lax.broadcasted_iota(jnp.int32, (1, LANES), 1)
    for head in range(heads):
        at = slice((3 * head + 2) * LANES, (3 * head + 3) * LANES)
        qrow[:, at] = jnp.where(lane == size, 1.0, qrow[:, at])
    pfull[row, lines(me, slot), :] = jnp.concatenate(
        [wp[...], jnp.zeros((slot - prows, quarter), bf16)], axis=0
    )
    for b in range(4):
        for d in range(8):
            pfull[b, d * slot + prows : (d + 1) * slot, :] = jnp.zeros((slot - prows, quarter), bf16)
    f1[lines(row, quarter), :] = w1[...]
    f2[lines(row, quarter), :] = w2[...]
    qmain[lines(row, quarter), :] = wq[:, :whole]

    spare = jnp.zeros((quarter, LANES - size), bf16)
    few = jnp.zeros((32, LANES - size), bf16)

    def widen(b):
        base = b * quarter
        at = pl.ds(pl.multiple_of(base, 32), quarter)
        for g in range(groups - 1):
            qwide[at, g * LANES : (g + 1) * LANES] = jnp.concatenate(
                [qmain[at, g * size : (g + 1) * size], spare], axis=1
            )
        for j in range(quarter // 32):
            some = pl.ds(pl.multiple_of(base + 32 * j, 32), 32)
            qwide[some, (groups - 1) * LANES :] = jnp.concatenate(
                [qmain[some, (groups - 1) * size :], qrest[b, :, j * rest : (j + 1) * rest], few],
                axis=1,
            )

    def q_wait(b):
        z_wait(0, b)
        z_wait(1, b)

    widen(row)
    first.event0()

    @pl.when(middle)
    def _():
        q_wait(other)
        forward_copy(0, 2, other).start()
        forward_copy(1, 2, other).start()

    q_wait(near)
    widen(near)
    first.event1()

    @pl.when(middle)
    def _():
        q_wait(far)
        forward_copy(0, 3, far).start()
        forward_copy(1, 3, far).start()

    first.event2()
    first.mate0()
    z_wait(2, near)

    def pcopy(i, r, at, count, block, to):
        ref = pfull.at[pl.ds(at, count), lines(block, slot)].at[:, pl.ds(0, prows)]
        return remote(ref, ref, psend.at[r, i], precv.at[r, i], col=to)

    def p_start(r, at):
        pcopy(0, r, at, 2, me, xn).start()
        pcopy(1, r, at, 2, me, yn).start()
        pcopy(2, r, at, 2, me, mate).start()

    def p_forward(r, at):
        pcopy(0, r, at, 2, xn, xn).wait_recv()
        pcopy(3, r, at, 1, xn, yn).start()
        pcopy(5, r, at, 2, xn, mate).start()
        pcopy(1, r, at, 2, yn, yn).wait_recv()
        pcopy(4, r, at + 1, 1, yn, xn).start()
        pcopy(6, r, at, 2, yn, mate).start()

    def p_last(r, at):
        pcopy(3, r, at, 1, dn, yn).wait_recv()
        pcopy(7, r, at, 1, dn, mate).start()
        pcopy(4, r, at + 1, 1, dn, xn).wait_recv()
        pcopy(8, r, at + 1, 1, dn, mate).start()

    def p_mates(r, at):
        pcopy(2, r, at, 2, mate, mate).wait_recv()
        pcopy(5, r, at, 2, xn + shift, mate).wait_recv()
        pcopy(6, r, at, 2, yn + shift, mate).wait_recv()
        pcopy(7, r, at, 1, dn + shift, mate).wait_recv()
        pcopy(8, r, at + 1, 1, dn + shift, mate).wait_recv()

    def p_finish(r, at):
        for i in (0, 1, 2, 5, 6):
            pcopy(i, r, at, 2, me, mate).wait_send()
        for i in (3, 4, 7, 8):
            pcopy(i, r, at, 1, me, mate).wait_send()

    p_start(0, lo)

    @pl.when(middle)
    def _():
        z_forward(2, 2, other)
        z_forward(2, 3, far)
        own_copy(3, 0).start()

    @pl.when(end)
    def _():
        q_wait(other)
        q_wait(far)

    widen(other)
    widen(far)
    first.mate1()
    first.mate2()

    factor = 1.4426950408889634 / size**0.5

    def qkv_block(i, c):
        @pl.when(i == 5)
        def _():
            p_forward(0, lo)

        at = lines(flipped(i))
        product = jnp.dot(x1[at, :], qwide[...], preferred_element_type=f32) + qrow[...]
        for g in range(groups):
            cols = slice(g * LANES, (g + 1) * LANES)
            value = product[:, cols]
            qkv[at, cols] = (value * factor if g % 3 == 0 else value).astype(bf16)
        return c

    lax.fori_loop(0, 8, qkv_block, 0)

    @pl.when(end)
    def _():
        z_wait(2, other)
        z_wait(2, far)

    p_start(1, hi)

    def a_copy(m, to):
        return remote(
            ctx_out.at[m], ctx.at[:, lines(me, slot)], asend.at[m], arecv.at[m], col=to
        )

    def attend_block(i, c):
        @pl.when(i == 1)
        def _():
            p_last(0, lo)

        @pl.when(i == 4)
        def _():
            p_forward(1, hi)

        @pl.when(i == 7)
        def _():
            p_last(1, hi)

        mask = 7 - i
        block = flipped(mask)
        at = lines(block)
        outs = []
        for head in range(heads):
            base = head * 3 * LANES
            query = qkv[at, base : base + LANES]
            keys = qkv[:, base + LANES : base + 2 * LANES]
            values = qkv[:, base + 2 * LANES : base + 3 * LANES]
            scores = lax.dot_general(
                query, keys, (((1,), (1,)), ((), ())), preferred_element_type=f32
            )
            top = jnp.max(scores, axis=-1, keepdims=True)
            expo = jnp.exp2(scores - top).astype(bf16)
            mixed = jnp.dot(expo, values, preferred_element_type=f32)
            outs.append(mixed[:, :size] / mixed[:, size : size + 1])
        outs.append(jnp.zeros((rows, slot - heads * size), f32))
        ctx_out[mask] = jnp.concatenate(outs, axis=1).astype(bf16)

        @pl.when(i < 7)
        def _():
            a_copy(mask, block).start()

        return c

    lax.fori_loop(0, 8, attend_block, 0)

    @pl.when(middle)
    def _():
        z_forward(3, 2, other)
        z_forward(3, 3, far)
        own_copy(4, 0).start()

    ctx[:, lines(me, slot)] = ctx_out[0]
    p_mates(0, lo)
    p_mates(1, hi)
    for m in range(1, 8):
        remote(
            ctx_out.at[m], ctx.at[:, lines(flipped(m), slot)], asend.at[m], arecv.at[m], col=mate
        ).wait_recv()

    for b in range(4):
        resid[:, b * quarter : (b + 1) * quarter] = jnp.dot(
            ctx[...], pfull[b], preferred_element_type=f32
        )

    def norm2(i, c):
        at = pl.ds(pl.multiple_of(i * chunk, chunk), chunk)
        to = pl.ds(pl.multiple_of(me * rows + i * chunk, chunk), chunk)
        value = tok[at, :].astype(f32) + resid[at, :] + vec[4:5, :]
        resid[at, :] = value
        x2[to, :] = norm(value, 2, 3).astype(bf16)
        return c

    lax.fori_loop(0, rows // chunk, norm2, 0)
    second = Gather(x2, 1)
    second.start()
    z_wait(3, near)
    second.event0()

    @pl.when(end)
    def _():
        z_wait(3, other)
        z_wait(3, far)

    def fc1_block(i, c):
        @pl.when(i == 1)
        def _():
            second.mate0()

        @pl.when(i == 2)
        def _():
            second.event1()

        @pl.when(i == 3)
        def _():
            second.mate1()

        @pl.when(i == 6)
        def _():
            second.event2()

        @pl.when(jnp.logical_and(i == 6, middle))
        def _():
            z_forward(4, 2, other)
            z_forward(4, 3, far)

        @pl.when(i == 7)
        def _():
            second.mate2()

        at = lines(flipped(i))
        value = jnp.dot(x2[at, :], f1[...], preferred_element_type=f32) + vec[7:8, :hidden]
        hid[at, :] = (0.5 * value * (1.0 + lax.erf(value * 0.7071067811865476))).astype(bf16)
        return c

    lax.fori_loop(0, 8, fc1_block, 0)

    starts = (
        (features - pieces[0]) * pair,
        pieces[0] - (pieces[0] - pieces[2]) * pair,
        (features - pieces[2]) * (1 - pair),
    )
    targets = (dn, yn, xn, me)

    class Piece:
        def __init__(self, p):
            self.p, self.width = p, pieces[p]
            self.cols = pl.ds(pl.multiple_of(starts[p], LANES), pieces[p])

        def copy(self, i, src, dst, to):
            return remote(src, dst, ssend.at[self.p, i], srecv.at[self.p, i], col=to)

        def of(self, ref, k, h):
            return ref.at[k, pl.ds(h * half, half), self.cols]

        def to_mate(self, k):
            block = flipped(6 - 2 * k + 1)
            return self.copy(k, part.at[lines(block), self.cols], mated.at[k, :, self.cols], mate)

        def compute(self):
            weight = f2.at[self.cols]

            def body(t, c):
                k = t % 4
                block = flipped(6 - 2 * k + 1 - t // 4)
                at = lines(block)
                part[at, self.cols] = project_back(hid[at, :], weight[...]).astype(bf16)

                @pl.when(t < 4)
                def _():
                    self.to_mate(k).start()

                return c

            lax.fori_loop(0, 8, body, 0)

        def mine(self, k, h):
            at = pl.ds(pl.multiple_of(targets[k] * rows + h * half, half), half)
            return part[at, self.cols].astype(f32) + mated[
                k, h * half : (h + 1) * half, self.cols
            ].astype(f32)

        def put(self, k, h, value):
            sums[k, h * half : (h + 1) * half, self.cols] = value.astype(bf16)

        def relays(self, h):
            return relay.at[h, :, self.cols]

        def c(self, i):
            k, h, dst, to = {
                4: (0, 0, self.relays(0), xn),
                5: (0, 1, self.relays(1), yn),
                6: (2, 0, self.of(landed, 0, 0), xn),
                7: (1, 1, self.of(landed, 1, 1), yn),
                8: (1, 0, self.of(landed, 1, 0), yn),
                9: (2, 1, self.of(landed, 0, 1), xn),
            }[i]
            return self.copy(i, self.of(sums, k, h), dst, to)

        def open(self):
            self.to_mate(0).wait_recv()
            self.put(0, 0, self.mine(0, 0))
            self.c(4).start()
            self.put(0, 1, self.mine(0, 1))
            self.c(5).start()
            self.to_mate(1).wait_recv()
            self.put(1, 1, self.mine(1, 1))
            self.c(7).start()
            self.to_mate(2).wait_recv()
            self.put(2, 0, self.mine(2, 0))
            self.c(6).start()

        def pass_on(self):
            self.c(4).wait_recv()
            self.put(1, 0, self.mine(1, 0) + relay[0, :, self.cols].astype(f32))
            self.c(8).start()
            self.c(5).wait_recv()
            self.put(2, 1, self.mine(2, 1) + relay[1, :, self.cols].astype(f32))
            self.c(9).start()

        def close(self):
            self.to_mate(3).wait_recv()
            for i in (6, 7, 8, 9):
                self.c(i).wait_recv()
            for h in (0, 1):
                at = slice(h * half, (h + 1) * half)
                total = (
                    self.mine(3, h)
                    + landed[0, at, self.cols].astype(f32)
                    + landed[1, at, self.cols].astype(f32)
                )
                value = resid[at, self.cols] + total + vec[5:6, self.cols]
                o_ref[at, self.cols] = value.astype(o_ref.dtype)

        def finish(self):
            for k in range(4):
                self.to_mate(k).wait_send()
            for i in range(4, 10):
                self.c(i).wait_send()

    one, two, three = Piece(0), Piece(1), Piece(2)
    z_wait(4, near)
    one.compute()
    one.open()

    @pl.when(end)
    def _():
        z_wait(4, other)

    two.compute()
    one.pass_on()
    two.open()

    @pl.when(end)
    def _():
        z_wait(4, far)

    three.compute()
    two.pass_on()
    three.open()
    one.close()
    three.pass_on()
    two.close()
    three.close()

    for piece in (one, two, three):
        piece.finish()
    first.finish()
    second.finish()
    p_finish(0, lo)
    p_finish(1, hi)
    for m in range(1, 8):
        a_copy(m, mate).wait_send()
    for w in range(5):
        for s in (0, 1):
            own_copy(w, s).wait_send()

    @pl.when(middle)
    def _():
        for w in range(5):
            forward_copy(w, 2, other).wait_send()
            forward_copy(w, 3, far).wait_send()


def layer_call(plan, tok, vec, wq, wp, w1, w2):
    rows, features, quarter = plan["rows"], plan["features"], plan["quarter"]
    hidden, slot = plan["hidden"], plan["slot"]
    wide = 3 * plan["heads"] * LANES
    length = 8 * rows
    bf16, f32 = jnp.bfloat16, jnp.float32
    dma = pltpu.SemaphoreType.DMA
    return pl.pallas_call(
        functools.partial(layer_kernel, plan),
        out_shape=jax.ShapeDtypeStruct((rows, features), bf16),
        in_specs=[pl.BlockSpec(memory_space=pltpu.VMEM)] * 6,
        out_specs=pl.BlockSpec(memory_space=pltpu.VMEM),
        scratch_shapes=[
            pltpu.VMEM((length, features), bf16),
            pltpu.VMEM((length, features), bf16),
            pltpu.VMEM((features, plan["whole"]), bf16),
            pltpu.VMEM((4, 32, quarter // 32 * plan["rest"]), bf16),
            pltpu.VMEM((features, wide), bf16),
            pltpu.VMEM((1, wide), f32),
            pltpu.VMEM((length, wide), bf16),
            pltpu.VMEM((rows, 8 * slot), bf16),
            pltpu.VMEM((8, rows, slot), bf16),
            pltpu.VMEM((4, 8 * slot, quarter), bf16),
            pltpu.VMEM((features, hidden), bf16),
            pltpu.VMEM((features, hidden), bf16),
            pltpu.VMEM((rows, features), f32),
            pltpu.VMEM((length, hidden), bf16),
            pltpu.VMEM((length, features), bf16),
            pltpu.VMEM((4, rows, features), bf16),
            pltpu.VMEM((3, rows, features), bf16),
            pltpu.VMEM((2, rows // 2, features), bf16),
            pltpu.VMEM((2, rows, features), bf16),
            dma((20,)), dma((20,)),
            dma((2, 14)), dma((2, 14)),
            dma((2, 9)), dma((2, 9)),
            dma((8,)), dma((8,)),
            dma((3, 10)), dma((3, 10)),
        ],
        compiler_params=pltpu.CompilerParams(
            collective_id=3, has_side_effects=True, vmem_limit_bytes=60 * 1024 * 1024
        ),
        name="layer",
    )(tok, vec, wq, wp, w1, w2)


def local(
    tokens_in,
    ln1_gain,
    ln1_bias,
    qkv_weight,
    qkv_bias,
    proj_weight,
    proj_bias,
    ln2_gain,
    ln2_bias,
    fc1_weight,
    fc1_bias,
    fc2_weight,
    fc2_bias,
):
    local_heads = HEADS // lax.axis_size("col")
    own_rows, features = tokens_in.shape
    size = qkv_weight.shape[1] // (3 * local_heads)
    padded = -(-(size + 1) // LANES) * LANES
    plan = fast_plan(
        local_heads, own_rows, features, qkv_weight.shape[1], proj_weight.shape[0],
        fc1_weight.shape[1],
    )
    if plan is not None:
        wide = lambda v: jnp.pad(v.astype(jnp.float32), (0, features - v.shape[0]))
        vec = jnp.stack(
            [
                wide(v)
                for v in (
                    ln1_gain, ln1_bias, ln2_gain, ln2_bias, proj_bias, fc2_bias, qkv_bias, fc1_bias
                )
            ]
        )
        return layer_call(plan, tokens_in, vec, qkv_weight, proj_weight, fc1_weight, fc2_weight)
    inputs = tokens_in.astype(jnp.float32)
    qkv_full = gather_row(qkv_weight, 0)
    proj_full = gather_row(proj_weight, 1)
    fc1_full = gather_row(fc1_weight, 0)
    fc2_full = gather_row(fc2_weight, 0)
    fc1_shift = fc1_bias.astype(jnp.float32)

    spare = padded - size
    qkv_wide = jnp.pad(
        qkv_full.reshape(features, local_heads, 3, size), ((0, 0), (0, 0), (0, 0), (0, spare))
    ).reshape(features, local_heads * 3 * padded)
    shift = jnp.pad(
        qkv_bias.astype(jnp.float32).reshape(local_heads, 3, size), ((0, 0), (0, 0), (0, spare))
    )
    shift = shift.at[:, 2, size].set(1.0).reshape(-1)
    scale = jnp.ones((local_heads, 3, padded), jnp.float32)
    scale = scale.at[:, 0].set(1.4426950408889634 / size**0.5).reshape(-1)

    ln1 = norm_local(inputs, ln1_gain, ln1_bias).astype(jnp.bfloat16)
    product = jnp.dot(gather_col(ln1, 0), qkv_wide, preferred_element_type=jnp.float32)
    qkv = ((product + shift) * scale).astype(jnp.bfloat16)
    attn = attend(qkv, local_heads, size, padded)
    proj_whole = cube_gather_col(proj_full)
    own_heads = lax.all_to_all(attn, "col", split_axis=0, concat_axis=1, tiled=True)
    attn_sum = jnp.dot(own_heads, proj_whole, preferred_element_type=jnp.float32)
    resid = inputs + attn_sum + proj_bias.astype(jnp.float32)
    ln2 = norm_local(resid, ln2_gain, ln2_bias).astype(jnp.bfloat16)
    product = jnp.dot(gather_col(ln2, 1), fc1_full, preferred_element_type=jnp.float32) + fc1_shift
    hidden = jax.nn.gelu(product, approximate=False).astype(jnp.bfloat16)
    mlp_sum = scatter_col(project_back(hidden, fc2_full).astype(jnp.bfloat16), 2)
    result = resid + mlp_sum + fc2_bias.astype(jnp.float32)
    return result.astype(jnp.bfloat16)


def solution(mesh):
    in_specs = (
        P(("row", "col"), None),
        P(),
        P(),
        P("row", "col"),
        P("col"),
        P("col", "row"),
        P(),
        P(),
        P(),
        P("row", "col"),
        P("col"),
        P("row", "col"),
        P(),
    )
    out_specs = P(("row", "col"), None)
    return jax.shard_map(local, mesh=mesh, in_specs=in_specs, out_specs=out_specs, check_vma=False)
```

profile of v0, /device:TPU:0, one launch (start us, length us, event | category | flops | bytes accessed | tf_op | source)
XLA Modules:
  0.0 152.6 jit_solution(4892281577075675314)
XLA Ops:
  0.0 0.7 pad.10
  0.7 0.0 copy-start.6
  0.7 0.7 copy-done.6
  1.4 0.0 copy-start
  1.4 0.7 copy-done
  2.1 0.0 copy-start.1
  2.1 0.7 copy-done.1
  2.7 0.0 copy-start.2
  2.8 0.7 copy-done.2
  3.4 0.0 copy-start.3
  3.4 0.7 copy-done.3
  4.1 0.0 copy-start.4
  4.1 0.7 copy-done.4
  4.8 0.0 copy-start.5
  4.8 0.7 copy-done.5
  5.5 0.1 stack.45
  5.6 0.6 stack.46.vec
  6.2 2.0 %copy.14.wq = bf16[352,528]{1,0:T(8,128)(2,1)} copy(bf16[352,528]{0,1:T(8,128)(2,1)} %param.16) | data formatting | bytes 743424 | tf_op args[3]
  8.2 142.4 %layer.1 = bf16[256,1408]{1,0:T(8,128)(2,1)} custom-call(bf16[256,1408]{1,0:T(8,128)(2,1)} %tok.1, f32[8,1408]{1,0:T(8,128)} %stack.46.vec, bf16[352,528]{1,0:T(8,128)(2,1)} %copy.14.wq, bf16[176,352]{1,0:T(8,128)(2,1)} %wp.1, bf16[352,768]{1,0:T(8,128)(2,1)} %w1.1, bf16[352,768]{1,0:T(8,128)(2,1)} %w2.1), custom_call_target="tpu_custom_call" | custom-call | tf_op jit(solution)/shard_map/layer/pallas_call | solution.py:903
  150.6 2.0 %copy.16 = bf16[256,1408]{1,0:T(8,128)(2,1)} copy(bf16[256,1408]{1,0:T(8,128)(2,1)} %layer.1) | data formatting | bytes 1441792
  (9 shorter events, 0.1 us)
Async XLA Ops:
  0.7 0.7 copy-start.6
  1.4 0.7 copy-start
  2.1 0.7 copy-start.1
  2.7 0.7 copy-start.2
  3.4 0.7 copy-start.3
  4.1 0.7 copy-start.4
  4.8 0.7 copy-start.5
where the time goes:
time: 153 us
  Pallas kernels  142 us (93%)
  local copies, waits for them, and re-layouts  9.54 us (6%)
    pallas_call x1, Pallas kernels, layer_call(): pl.pallas_call(functools.partial(layer_kernel, plan), out_shape=jax.Shape...  142 us
    unnamed x16, local copies, waits for them, and re-layouts  8.72 us

commit v1 on v0

--- a/solution.py
+++ b/solution.py
@@ -305,37 +305,40 @@
     whole = qkv_width // LANES * LANES
     rest = qkv_width - whole
     ok = (
-        own_rows % 32 == 0 and features % LANES == 0 and quarter % 32 == 0
+        hidden == 3 * heads * LANES and own_rows % 32 == 0 and features % LANES == 0 and quarter % 32 == 0
         and hidden % LANES == 0 and 0 < rest and proj_rows == heads * size
-        and proj_rows % 16 == 0 and size < LANES and whole // size == 3 * heads - 1
+        and proj_rows % 16 == 0 and 0 < proj_rows - LANES <= LANES // 2
+        and 8 * proj_rows == features and size < LANES and whole // size == 3 * heads - 1
     )
     if not ok:
         return None
     first = 2 * quarter // LANES * LANES
     last = -(-quarter // LANES) * LANES
     middle = features - first - last
-    if middle <= 0 or features - last > 3 * quarter:
+    if middle <= 0 or last <= LANES or features - last > 3 * quarter:
         return None
     return dict(
         heads=heads, size=size, rows=own_rows, features=features, quarter=quarter, whole=whole,
-        rest=rest, proj_rows=proj_rows, slot=-(-proj_rows // LANES) * LANES, hidden=hidden,
-        pieces=(first, middle, last),
+        rest=rest, proj_rows=proj_rows, hidden=hidden,
+        pieces=(first, middle, last - LANES, LANES),
     )
 
 
 def layer_kernel(
-    plan, tok, vec, wq, wp, w1, w2, o_ref,
-    x1, x2, qmain, qrest, qwide, qrow, qkv, ctx, ctx_out, pfull, f1, f2, resid, hid, part,
+    plan, tok_in, g1, c1, qb, pb, g2, c2, d1, d2, wq_in, wp, w1, w2, o_ref,
+    tok, wq, v1, v2, v3, v4, v5, v6, v7, v8,
+    vec, x1, x2, qmain, qrest, qwide, qrow, qkv, ctx, heads_out, tails_out, heads_in, tails_in, pfull, f1, f2, resid,
     mated, sums, relay, landed,
-    zsend, zrecv, gsend, grecv, psend, precv, asend, arecv, ssend, srecv,
+    lsem, zsend, zrecv, gsend, grecv, psend, precv, asend, arecv, ssend, srecv,
 ):
     heads, size, rows = plan["heads"], plan["size"], plan["rows"]
     features, quarter = plan["features"], plan["quarter"]
-    whole, rest, slot, prows = plan["whole"], plan["rest"], plan["slot"], plan["proj_rows"]
+    whole, rest, prows = plan["whole"], plan["rest"], plan["proj_rows"]
     hidden, pieces = plan["hidden"], plan["pieces"]
     half = rows // 2
     groups = 3 * heads
     f32, bf16 = jnp.float32, jnp.bfloat16
+    hid, part = qkv, x1
 
     row = lax.axis_index("row")
     me, mate, xn, yn, dn = neighbours()
@@ -363,6 +366,9 @@
             barrier, inc=1, device_id={"row": (row + step) % 4}, device_id_type=MESH
         )
 
+    def load(i, src, dst):
+        return pltpu.make_async_copy(src, dst, lsem.at[i])
+
     def remote(src, dst, ssem, rsem, **to):
         return pltpu.make_async_remote_copy(
             src_ref=src, dst_ref=dst, send_sem=ssem, recv_sem=rsem,
@@ -371,6 +377,13 @@
 
     def lines(b, n=rows):
         return pl.ds(pl.multiple_of(b * n, n), n)
+
+    def cut(w, b):
+        low = b // 2
+        return (1 - low) * LANES if w == 5 else low * (quarter - LANES)
+
+    def length_of(w):
+        return quarter - LANES if w == 5 else LANES
 
     def place(w, b):
         if w == 0:
@@ -378,40 +391,70 @@
         if w == 1:
             return qrest.at[b]
         if w == 2:
-            return pfull.at[b, lines(me, slot)].at[pl.ds(0, prows)]
-        return (f1 if w == 3 else f2).at[lines(b, quarter)]
+            return pfull.at[b, lines(me, prows)]
+        if w == 3:
+            return f1.at[lines(b, quarter)]
+        if w == 4:
+            return f2.at[lines(b, quarter)]
+        return f2.at[pl.ds(pl.multiple_of(b * quarter + cut(w, b), 32), length_of(w))]
 
     def source(w):
         if w == 0:
-            return wq.at[:, pl.ds(0, whole)]
+            return place(0, row)
         return (None, qrest.at[row], wp, w1, w2)[w]
+
+    def z_copy(w, s, b):
+        return remote(
+            place(w, b), place(w, b), zsend.at[w * 5 + s], zrecv.at[w * 4 + b],
+            row=other if s in (1, 4) else near,
+        )
 
     def own_copy(w, s):
         return remote(
-            source(w), place(w, row), zsend.at[w * 4 + s], zrecv.at[w * 4 + row],
-            row=near if s == 0 else other,
+            source(w), place(w, row), zsend.at[w * 5 + s], zrecv.at[w * 4 + row],
+            row=other if s == 1 else near,
         )
 
-    def forward_copy(w, s, b):
-        return remote(
-            place(w, b), place(w, b), zsend.at[w * 4 + s], zrecv.at[w * 4 + b], row=near
-        )
-
     def z_wait(w, b):
-        remote(
-            place(w, b), place(w, b), zsend.at[w * 4], zrecv.at[w * 4 + b], row=near
-        ).wait_recv()
-
-    def z_forward(w, s, b):
+        z_copy(w, 0, b).wait_recv()
+
+    def z_forward(w, s):
+        b = {2: other, 3: far, 4: near}[s]
         z_wait(w, b)
-        forward_copy(w, s, b).start()
-
+        z_copy(w, s, b).start()
+
+    loads = [load(0, wq_in, wq), load(1, tok_in, tok)]
+    for i, (src, dst) in enumerate(
+        ((g1, v1), (c1, v2), (g2, v3), (c2, v4), (pb, v5), (d2, v6), (qb, v7), (d1, v8))
+    ):
+        loads.append(load(i + 2, src, dst))
+    loads.append(load(10, wp, place(2, row)))
+    loads.append(load(11, w1, place(3, row)))
+    loads.append(load(12, w2, place(4, row)))
+    for c in loads:
+        c.start()
+    loads[0].wait()
+    turned = wq[...].astype(f32).T.astype(bf16)
+    qmain[lines(row, quarter), :] = turned[:, :whole]
     for j in range(quarter // 32):
-        qrest[row, :, j * rest : (j + 1) * rest] = wq[32 * j : 32 * (j + 1), whole:]
+        qrest[row, :, j * rest : (j + 1) * rest] = turned[32 * j : 32 * (j + 1), whole:]
+    for i, v in enumerate((v1, v2, v3, v4, v5, v6, v7, v8)):
+        loads[i + 2].wait()
+        vec[i : i + 1, : v.shape[0]] = v[...].astype(f32).reshape(1, -1)
+    loads[1].wait()
     pl.semaphore_wait(barrier, 10)
-    for w in (0, 2):
-        for s in (0, 1):
-            own_copy(w, s).start()
+    for w in (0, 1, 2):
+        own_copy(w, 0).start()
+
+    @pl.when(middle)
+    def _():
+        for w in (0, 1, 2):
+            own_copy(w, 1).start()
+
+    @pl.when(end)
+    def _():
+        for w in (3, 4):
+            own_copy(w, 0).start()
 
     def norm(values, g, b):
         mean = jnp.mean(values, axis=-1, keepdims=True)
@@ -428,8 +471,6 @@
         return c
 
     lax.fori_loop(0, rows // chunk, norm1, 0)
-    for s in (0, 1):
-        own_copy(1, s).start()
 
     class Gather:
         def __init__(self, x, gi):
@@ -484,13 +525,6 @@
 
     first = Gather(x1, 0)
     first.start()
-    for w in (3, 4):
-        @pl.when(end)
-        def _():
-            own_copy(w, 0).start()
-
-        own_copy(w, 1).start()
-
     qrow[...] = jnp.zeros_like(qrow)
     for g in range(groups):
         qrow[:, g * LANES : g * LANES + size] = vec[6:7, g * size : (g + 1) * size]
@@ -498,15 +532,8 @@
     for head in range(heads):
         at = slice((3 * head + 2) * LANES, (3 * head + 3) * LANES)
         qrow[:, at] = jnp.where(lane == size, 1.0, qrow[:, at])
-    pfull[row, lines(me, slot), :] = jnp.concatenate(
-        [wp[...], jnp.zeros((slot - prows, quarter), bf16)], axis=0
-    )
-    for b in range(4):
-        for d in range(8):
-            pfull[b, d * slot + prows : (d + 1) * slot, :] = jnp.zeros((slot - prows, quarter), bf16)
-    f1[lines(row, quarter), :] = w1[...]
-    f2[lines(row, quarter), :] = w2[...]
-    qmain[lines(row, quarter), :] = wq[:, :whole]
+    for c in loads[10:]:
+        c.wait()
 
     spare = jnp.zeros((quarter, LANES - size), bf16)
     few = jnp.zeros((32, LANES - size), bf16)
@@ -525,35 +552,38 @@
                 axis=1,
             )
 
+    widen(row)
+
     def q_wait(b):
         z_wait(0, b)
         z_wait(1, b)
 
-    widen(row)
+    @pl.when(middle)
+    def _():
+        for w in (0, 1):
+            z_forward(w, 4)
+        for w in (0, 1):
+            z_forward(w, 2)
+
     first.event0()
 
+    @pl.when(end)
+    def _():
+        q_wait(near)
+
+    widen(near)
+
     @pl.when(middle)
     def _():
-        q_wait(other)
-        forward_copy(0, 2, other).start()
-        forward_copy(1, 2, other).start()
-
-    q_wait(near)
-    widen(near)
+        z_forward(2, 4)
+        own_copy(3, 1).start()
+        for w in (0, 1):
+            z_forward(w, 3)
+
     first.event1()
 
-    @pl.when(middle)
-    def _():
-        q_wait(far)
-        forward_copy(0, 3, far).start()
-        forward_copy(1, 3, far).start()
-
-    first.event2()
-    first.mate0()
-    z_wait(2, near)
-
     def pcopy(i, r, at, count, block, to):
-        ref = pfull.at[pl.ds(at, count), lines(block, slot)].at[:, pl.ds(0, prows)]
+        ref = pfull.at[pl.ds(at, count), lines(block, prows)]
         return remote(ref, ref, psend.at[r, i], precv.at[r, i], col=to)
 
     def p_start(r, at):
@@ -588,13 +618,23 @@
         for i in (3, 4, 7, 8):
             pcopy(i, r, at, 1, me, mate).wait_send()
 
+
+    @pl.when(end)
+    def _():
+        z_wait(2, near)
+
     p_start(0, lo)
 
     @pl.when(middle)
     def _():
-        z_forward(2, 2, other)
-        z_forward(2, 3, far)
+        z_forward(2, 2)
+        z_forward(2, 3)
         own_copy(3, 0).start()
+        z_forward(3, 4)
+        own_copy(4, 1).start()
+
+    first.event2()
+    first.mate0()
 
     @pl.when(end)
     def _():
@@ -609,9 +649,18 @@
     factor = 1.4426950408889634 / size**0.5
 
     def qkv_block(i, c):
-        @pl.when(i == 5)
+        @pl.when(i == 6)
         def _():
             p_forward(0, lo)
+
+        @pl.when(jnp.logical_and(i == 7, end))
+        def _():
+            z_wait(2, other)
+            z_wait(2, far)
+
+        @pl.when(i == 7)
+        def _():
+            p_start(1, hi)
 
         at = lines(flipped(i))
         product = jnp.dot(x1[at, :], qwide[...], preferred_element_type=f32) + qrow[...]
@@ -623,16 +672,18 @@
 
     lax.fori_loop(0, 8, qkv_block, 0)
 
-    @pl.when(end)
-    def _():
-        z_wait(2, other)
-        z_wait(2, far)
-
-    p_start(1, hi)
-
-    def a_copy(m, to):
-        return remote(
-            ctx_out.at[m], ctx.at[:, lines(me, slot)], asend.at[m], arecv.at[m], col=to
+    rest_lanes = prows - LANES
+
+    def a_copies(i, core, m, to):
+        at = lines(core)
+        tail = pl.ds(pl.multiple_of(core * half, half), half)
+        return (
+            remote(
+                heads_out.at[i, at], heads_in.at[me], asend.at[0, m], arecv.at[0, m], col=to
+            ),
+            remote(
+                tails_out.at[i, tail], tails_in.at[me], asend.at[1, m], arecv.at[1, m], col=to
+            ),
         )
 
     def attend_block(i, c):
@@ -640,54 +691,88 @@
         def _():
             p_last(0, lo)
 
-        @pl.when(i == 4)
+        @pl.when(jnp.logical_and(i == 1, middle))
+        def _():
+            z_forward(3, 2)
+            z_wait(4, near)
+            for w in (5, 6):
+                z_copy(w, 4, near).start()
+
+        @pl.when(i == 3)
         def _():
             p_forward(1, hi)
 
-        @pl.when(i == 7)
-        def _():
-            p_last(1, hi)
-
-        mask = 7 - i
-        block = flipped(mask)
-        at = lines(block)
+        chip = flipped(6 - 2 * i) // 2
+        at = lines(chip, 2 * rows)
+        scores = []
+        for head in range(heads):
+            base = head * 3 * LANES
+            scores.append(
+                lax.dot_general(
+                    qkv[at, base : base + LANES], qkv[:, base + LANES : base + 2 * LANES],
+                    (((1,), (1,)), ((), ())), preferred_element_type=f32,
+                )
+            )
+        expos = [
+            jnp.exp2(x - jnp.max(x, axis=-1, keepdims=True)).astype(bf16) for x in scores
+        ]
         outs = []
         for head in range(heads):
-            base = head * 3 * LANES
-            query = qkv[at, base : base + LANES]
-            keys = qkv[:, base + LANES : base + 2 * LANES]
-            values = qkv[:, base + 2 * LANES : base + 3 * LANES]
-            scores = lax.dot_general(
-                query, keys, (((1,), (1,)), ((), ())), preferred_element_type=f32
+            base = (head * 3 + 2) * LANES
+            mixed = jnp.dot(
+                expos[head], qkv[:, base : base + LANES], preferred_element_type=f32
             )
-            top = jnp.max(scores, axis=-1, keepdims=True)
-            expo = jnp.exp2(scores - top).astype(bf16)
-            mixed = jnp.dot(expo, values, preferred_element_type=f32)
             outs.append(mixed[:, :size] / mixed[:, size : size + 1])
-        outs.append(jnp.zeros((rows, slot - heads * size), f32))
-        ctx_out[mask] = jnp.concatenate(outs, axis=1).astype(bf16)
-
-        @pl.when(i < 7)
-        def _():
-            a_copy(mask, block).start()
+        mixed = jnp.concatenate(outs, axis=1).astype(bf16)
+        gap = jnp.zeros((half, LANES // 2 - rest_lanes), bf16)
+        heads_out[i] = mixed[:, :LANES]
+        for core in (0, 1):
+            top, low = (
+                mixed[core * rows + h * half : core * rows + (h + 1) * half, LANES:]
+                for h in (0, 1)
+            )
+            tails_out[i, core * half : (core + 1) * half, :] = jnp.concatenate(
+                [top, gap, low, gap], axis=1
+            )
+        for core in (0, 1):
+            to = 2 * chip + core
+
+            @pl.when(to != me)
+            def _():
+                for c in a_copies(i, core, 6 - 2 * i + (core + me) % 2, to):
+                    c.start()
 
         return c
 
-    lax.fori_loop(0, 8, attend_block, 0)
-
+    lax.fori_loop(0, 4, attend_block, 0)
     @pl.when(middle)
     def _():
-        z_forward(3, 2, other)
-        z_forward(3, 3, far)
+        z_forward(3, 3)
         own_copy(4, 0).start()
 
-    ctx[:, lines(me, slot)] = ctx_out[0]
+    p_last(1, hi)
+    first.finish()
+    heads_in[me] = heads_out[3, lines(me % 2), :]
+    tails_in[me] = tails_out[3, lines(me % 2, half), :]
     p_mates(0, lo)
     p_mates(1, hi)
     for m in range(1, 8):
-        remote(
-            ctx_out.at[m], ctx.at[:, lines(flipped(m), slot)], asend.at[m], arecv.at[m], col=mate
-        ).wait_recv()
+        for ref, out, n, which in (
+            (heads_in, heads_out, rows, 0), (tails_in, tails_out, half, 1)
+        ):
+            arrived = remote(
+                out.at[0, pl.ds(0, n)], ref.at[flipped(m)], asend.at[which, m],
+                arecv.at[which, m], col=mate,
+            )
+            arrived.wait_recv()
+
+    for d in range(8):
+        base = d * prows
+        ctx[:, base : base + LANES] = heads_in[d]
+        for h in (0, 1):
+            ctx[h * half : (h + 1) * half, base + LANES : base + prows] = tails_in[
+                d, :, h * (LANES // 2) : h * (LANES // 2) + rest_lanes
+            ]
 
     for b in range(4):
         resid[:, b * quarter : (b + 1) * quarter] = jnp.dot(
@@ -705,52 +790,18 @@
     lax.fori_loop(0, rows // chunk, norm2, 0)
     second = Gather(x2, 1)
     second.start()
-    z_wait(3, near)
     second.event0()
 
     @pl.when(end)
     def _():
+        z_wait(3, near)
         z_wait(3, other)
         z_wait(3, far)
 
-    def fc1_block(i, c):
-        @pl.when(i == 1)
-        def _():
-            second.mate0()
-
-        @pl.when(i == 2)
-        def _():
-            second.event1()
-
-        @pl.when(i == 3)
-        def _():
-            second.mate1()
-
-        @pl.when(i == 6)
-        def _():
-            second.event2()
-
-        @pl.when(jnp.logical_and(i == 6, middle))
-        def _():
-            z_forward(4, 2, other)
-            z_forward(4, 3, far)
-
-        @pl.when(i == 7)
-        def _():
-            second.mate2()
-
-        at = lines(flipped(i))
-        value = jnp.dot(x2[at, :], f1[...], preferred_element_type=f32) + vec[7:8, :hidden]
-        hid[at, :] = (0.5 * value * (1.0 + lax.erf(value * 0.7071067811865476))).astype(bf16)
-        return c
-
-    lax.fori_loop(0, 8, fc1_block, 0)
-
-    starts = (
-        (features - pieces[0]) * pair,
-        pieces[0] - (pieces[0] - pieces[2]) * pair,
-        (features - pieces[2]) * (1 - pair),
-    )
+    starts, done = [], 0
+    for width in pieces:
+        starts.append(done + (features - width - 2 * done) * pair)
+        done += width
     targets = (dn, yn, xn, me)
 
     class Piece:
@@ -768,22 +819,22 @@
             block = flipped(6 - 2 * k + 1)
             return self.copy(k, part.at[lines(block), self.cols], mated.at[k, :, self.cols], mate)
 
-        def compute(self):
+        def compute(self, stage):
             weight = f2.at[self.cols]
 
             def body(t, c):
-                k = t % 4
-                block = flipped(6 - 2 * k + 1 - t // 4)
+                k = 2 - t % 2 if stage == 0 else 3 * (t % 2)
+                block = flipped(6 - 2 * k + 1 - t // 2)
                 at = lines(block)
                 part[at, self.cols] = project_back(hid[at, :], weight[...]).astype(bf16)
 
-                @pl.when(t < 4)
+                @pl.when(t < 2)
                 def _():
                     self.to_mate(k).start()
 
                 return c
 
-            lax.fori_loop(0, 8, body, 0)
+            lax.fori_loop(0, 4, body, 0)
 
         def mine(self, k, h):
             at = pl.ds(pl.multiple_of(targets[k] * rows + h * half, half), half)
@@ -808,18 +859,20 @@
             }[i]
             return self.copy(i, self.of(sums, k, h), dst, to)
 
-        def open(self):
+        def open_direct(self):
+            self.to_mate(2).wait_recv()
+            self.put(2, 0, self.mine(2, 0))
+            self.c(6).start()
+            self.to_mate(1).wait_recv()
+            self.put(1, 1, self.mine(1, 1))
+            self.c(7).start()
+
+        def open_relayed(self):
             self.to_mate(0).wait_recv()
             self.put(0, 0, self.mine(0, 0))
             self.c(4).start()
             self.put(0, 1, self.mine(0, 1))
             self.c(5).start()
-            self.to_mate(1).wait_recv()
-            self.put(1, 1, self.mine(1, 1))
-            self.c(7).start()
-            self.to_mate(2).wait_recv()
-            self.put(2, 0, self.mine(2, 0))
-            self.c(6).start()
 
         def pass_on(self):
             self.c(4).wait_recv()
@@ -849,63 +902,135 @@
             for i in range(4, 10):
                 self.c(i).wait_send()
 
-    one, two, three = Piece(0), Piece(1), Piece(2)
-    z_wait(4, near)
-    one.compute()
-    one.open()
+    one, two, three, four = (Piece(p) for p in range(4))
+
+    def fc1_block(i, c):
+        @pl.when(i == 1)
+        def _():
+            second.mate0()
+
+        @pl.when(i == 2)
+        def _():
+            second.event1()
+
+        @pl.when(i == 3)
+        def _():
+            second.mate1()
+
+        @pl.when(i == 6)
+        def _():
+            second.event2()
+
+        @pl.when(jnp.logical_and(i == 2, middle))
+        def _():
+            z_forward(4, 2)
+
+        @pl.when(jnp.logical_and(i == 5, middle))
+        def _():
+            z_forward(5, 3)
+            z_forward(6, 3)
+
+        @pl.when(i == 7)
+        def _():
+            second.mate2()
+
+        at = lines(flipped(i))
+        for c0 in range(0, hidden, 2 * LANES):
+            cols = slice(c0, c0 + 2 * LANES)
+            value = jnp.dot(x2[at, :], f1[:, cols], preferred_element_type=f32) + vec[7:8, cols]
+            hid[at, cols] = (
+                0.5 * value * (1.0 + lax.erf(value * 0.7071067811865476))
+            ).astype(bf16)
+
+        @pl.when(jnp.logical_and(i == 5, end))
+        def _():
+            z_wait(4, near)
+
+        @pl.when(i == 5)
+        def _():
+            one.compute(0)
+            one.open_direct()
+
+        return c
+
+    lax.fori_loop(0, 8, fc1_block, 0)
+
+    one.compute(1)
+    one.open_relayed()
 
     @pl.when(end)
     def _():
         z_wait(4, other)
 
-    two.compute()
+    two.compute(0)
+    two.open_direct()
+    two.compute(1)
+    two.open_relayed()
     one.pass_on()
-    two.open()
 
     @pl.when(end)
     def _():
-        z_wait(4, far)
-
-    three.compute()
+        z_wait(5, far)
+
+    three.compute(0)
+    three.open_direct()
+    three.compute(1)
+    three.open_relayed()
     two.pass_on()
-    three.open()
     one.close()
+
+    @pl.when(end)
+    def _():
+        z_wait(6, far)
+
+    four.compute(0)
+    four.open_direct()
+    four.compute(1)
+    four.open_relayed()
     three.pass_on()
     two.close()
+    four.pass_on()
     three.close()
-
-    for piece in (one, two, three):
+    four.close()
+
+    for piece in (one, two, three, four):
         piece.finish()
-    first.finish()
     second.finish()
     p_finish(0, lo)
     p_finish(1, hi)
     for m in range(1, 8):
-        a_copy(m, mate).wait_send()
+        for c in a_copies(0, 0, m, mate):
+            c.wait_send()
     for w in range(5):
-        for s in (0, 1):
-            own_copy(w, s).wait_send()
+        own_copy(w, 0).wait_send()
 
     @pl.when(middle)
     def _():
         for w in range(5):
-            forward_copy(w, 2, other).wait_send()
-            forward_copy(w, 3, far).wait_send()
-
-
-def layer_call(plan, tok, vec, wq, wp, w1, w2):
+            own_copy(w, 1).wait_send()
+            z_copy(w, 2, other).wait_send()
+        for w in (0, 1, 2, 3, 5, 6):
+            z_copy(w, 3, far).wait_send()
+            z_copy(w, 4, near).wait_send()
+
+
+def layer_call(plan, *arrays):
     rows, features, quarter = plan["rows"], plan["features"], plan["quarter"]
-    hidden, slot = plan["hidden"], plan["slot"]
+    hidden = plan["hidden"]
     wide = 3 * plan["heads"] * LANES
     length = 8 * rows
     bf16, f32 = jnp.bfloat16, jnp.float32
     dma = pltpu.SemaphoreType.DMA
     return pl.pallas_call(
         functools.partial(layer_kernel, plan),
-        out_shape=jax.ShapeDtypeStruct((rows, features), bf16),
-        in_specs=[pl.BlockSpec(memory_space=pltpu.VMEM)] * 6,
+        out_shape=jax.ShapeDtypeStruct((rows, features), f32),
+        in_specs=[pl.BlockSpec(memory_space=pl.ANY)] * 13,
         out_specs=pl.BlockSpec(memory_space=pltpu.VMEM),
         scratch_shapes=[
+            pltpu.VMEM((rows, features), bf16),
+            pltpu.VMEM(arrays[9].shape, bf16),
+            *(pltpu.VMEM(arrays[i].shape, bf16) for i in (1, 2, 5, 6, 4, 8, 3, 7)),
+            pltpu.VMEM((8, features), f32),
             pltpu.VMEM((length, features), bf16),
             pltpu.VMEM((length, features), bf16),
             pltpu.VMEM((features, plan["whole"]), bf16),
@@ -913,29 +1038,31 @@
             pltpu.VMEM((features, wide), bf16),
             pltpu.VMEM((1, wide), f32),
             pltpu.VMEM((length, wide), bf16),
-            pltpu.VMEM((rows, 8 * slot), bf16),
-            pltpu.VMEM((8, rows, slot), bf16),
-            pltpu.VMEM((4, 8 * slot, quarter), bf16),
+            pltpu.VMEM((rows, features), bf16),
+            pltpu.VMEM((4, 2 * rows, LANES), bf16),
+            pltpu.VMEM((4, rows, LANES), bf16),
+            pltpu.VMEM((8, rows, LANES), bf16),
+            pltpu.VMEM((8, rows // 2, LANES), bf16),
+            pltpu.VMEM((4, features, quarter), bf16),
             pltpu.VMEM((features, hidden), bf16),
             pltpu.VMEM((features, hidden), bf16),
             pltpu.VMEM((rows, features), f32),
-            pltpu.VMEM((length, hidden), bf16),
-            pltpu.VMEM((length, features), bf16),
             pltpu.VMEM((4, rows, features), bf16),
             pltpu.VMEM((3, rows, features), bf16),
             pltpu.VMEM((2, rows // 2, features), bf16),
             pltpu.VMEM((2, rows, features), bf16),
-            dma((20,)), dma((20,)),
+            dma((13,)),
+            dma((35,)), dma((28,)),
             dma((2, 14)), dma((2, 14)),
             dma((2, 9)), dma((2, 9)),
-            dma((8,)), dma((8,)),
-            dma((3, 10)), dma((3, 10)),
+            dma((2, 8)), dma((2, 8)),
+            dma((4, 10)), dma((4, 10)),
         ],
         compiler_params=pltpu.CompilerParams(
             collective_id=3, has_side_effects=True, vmem_limit_bytes=60 * 1024 * 1024
         ),
         name="layer",
-    )(tok, vec, wq, wp, w1, w2)
+    )(*arrays)
 
 
 def local(
@@ -962,16 +1089,10 @@
         fc1_weight.shape[1],
     )
     if plan is not None:
-        wide = lambda v: jnp.pad(v.astype(jnp.float32), (0, features - v.shape[0]))
-        vec = jnp.stack(
-            [
-                wide(v)
-                for v in (
-                    ln1_gain, ln1_bias, ln2_gain, ln2_bias, proj_bias, fc2_bias, qkv_bias, fc1_bias
-                )
-            ]
-        )
-        return layer_call(plan, tokens_in, vec, qkv_weight, proj_weight, fc1_weight, fc2_weight)
+        return layer_call(
+            plan, tokens_in, ln1_gain, ln1_bias, qkv_bias, proj_bias, ln2_gain, ln2_bias, fc1_bias,
+            fc2_bias, qkv_weight.T, proj_weight, fc1_weight, fc2_weight,
+        ).astype(jnp.bfloat16)
     inputs = tokens_in.astype(jnp.float32)
     qkv_full = gather_row(qkv_weight, 0)
     proj_full = gather_row(proj_weight, 1)

time: 153 us -> 128 us (0.84)
  Pallas kernels: 142 us -> 126 us
  local copies, waits for them, and re-layouts: 9.54 us -> 0 us
  other arithmetic: 0.62 us -> 2.3 us
    pallas_call x1, Pallas kernels: 142 us -> 126 us  [layer_call(): pl.pallas_call(functools.partial(layer_kernel, plan), out_shape=jax.Shape...]
    unnamed x16 -> x0, local copies, waits for them, and re-layouts: 8.72 us -> none
    convert_element_type x0 -> x1, other arithmetic: none -> 2.3 us  [local(): return layer_call(plan, tokens_in, ln1_gain, ln1_bias, qkv_bias, proj_bia...]
where the time goes in v1:
time: 128 us
  Pallas kernels  126 us (98%)
  other arithmetic  2.3 us (2%)
    pallas_call x1, Pallas kernels, layer_call(): pl.pallas_call(functools.partial(layer_kernel, plan), out_shape=jax.Shape...  126 us

profile of v1, /device:TPU:0, one launch (start us, length us, event | category | flops | bytes accessed | tf_op | source)
XLA Modules:
  0.0 128.0 jit_solution(7109822781074049114)
XLA Ops:
  0.0 125.7 %layer.1 = f32[256,1408]{1,0:T(8,128)} custom-call(bf16[256,1408]{1,0:T(8,128)(2,1)} %tok_in.1, bf16[1408]{0:T(1024)(128)(2,1)} %g1.1, bf16[1408]{0:T(1024)(128)(2,1)} %c1.1, bf16[528]{0:T(1024)(128)(2,1)} %qb.1, bf16[1408]{0:T(1024)(128)(2,1)} %pb.1, bf16[1408]{0:T(1024)(128)(2,1)} %g2.1, bf16[1408]{0:T(1024)(128)(2,1)} %c2.1, bf16[768]{0:T(1024)(128)(2,1)} %d1.1, ...), custom_call_target="tpu_custom_call" | custom-call | tf_op jit(solution)/shard_map/layer/pallas_call | solution.py:1024
  125.7 2.3 %convert_element_type.3 = bf16[256,1408]{1,0:T(8,128)(2,1)} convert(f32[256,1408]{1,0:T(8,128)} %layer.1) | non-fusion elementwise | flops 360448 | bytes 2162688 | tf_op jit(solution)/shard_map/convert_element_type | solution.py:1095

commit v2 on v1

--- a/solution.py
+++ b/solution.py
@@ -315,12 +315,15 @@
     first = 2 * quarter // LANES * LANES
     last = -(-quarter // LANES) * LANES
     middle = features - first - last
-    if middle <= 0 or last <= LANES or features - last > 3 * quarter:
+    if middle <= LANES or last <= LANES or features - last > 3 * quarter:
+        return None
+    if (first + middle - LANES - 2 * quarter) % 32:
         return None
     return dict(
         heads=heads, size=size, rows=own_rows, features=features, quarter=quarter, whole=whole,
         rest=rest, proj_rows=proj_rows, hidden=hidden,
-        pieces=(first, middle, last - LANES, LANES),
+        pieces=(first, middle - LANES, LANES, last - LANES, LANES),
+        early=first + middle - LANES - 2 * quarter,
     )
 
 
@@ -329,7 +332,7 @@
     tok, wq, v1, v2, v3, v4, v5, v6, v7, v8,
     vec, x1, x2, qmain, qrest, qwide, qrow, qkv, ctx, heads_out, tails_out, heads_in, tails_in, pfull, f1, f2, resid,
     mated, sums, relay, landed,
-    lsem, zsend, zrecv, gsend, grecv, psend, precv, asend, arecv, ssend, srecv,
+    lsem, osem, zsend, zrecv, gsend, grecv, psend, precv, asend, arecv, ssend, srecv,
 ):
     heads, size, rows = plan["heads"], plan["size"], plan["rows"]
     features, quarter = plan["features"], plan["quarter"]
@@ -361,10 +364,12 @@
         pl.semaphore_signal(
             barrier, inc=1, device_id={"col": flipped(step)}, device_id_type=MESH
         )
-    for step in range(1, 4):
-        pl.semaphore_signal(
-            barrier, inc=1, device_id={"row": (row + step) % 4}, device_id_type=MESH
-        )
+    pl.semaphore_signal(barrier, inc=1, device_id={"row": near}, device_id_type=MESH)
+
+    @pl.when(middle)
+    def _():
+        pl.semaphore_signal(barrier, inc=1, device_id={"row": other}, device_id_type=MESH)
+
 
     def load(i, src, dst):
         return pltpu.make_async_copy(src, dst, lsem.at[i])
@@ -378,12 +383,19 @@
     def lines(b, n=rows):
         return pl.ds(pl.multiple_of(b * n, n), n)
 
+    early = plan["early"]
+
     def cut(w, b):
         low = b // 2
-        return (1 - low) * LANES if w == 5 else low * (quarter - LANES)
+        return {
+            5: (1 - low) * LANES,
+            6: low * (quarter - LANES),
+            7: (1 - low) * (quarter - early),
+            8: low * early,
+        }[w]
 
     def length_of(w):
-        return quarter - LANES if w == 5 else LANES
+        return {5: quarter - LANES, 6: LANES, 7: early, 8: quarter - early}[w]
 
     def place(w, b):
         if w == 0:
@@ -403,25 +415,36 @@
             return place(0, row)
         return (None, qrest.at[row], wp, w1, w2)[w]
 
+    zwhich = (0, 1, 1, 2, 2)
+
+    def zslot(w, which):
+        return w * 3 + which if w < 5 else 10 + w
+
     def z_copy(w, s, b):
         return remote(
-            place(w, b), place(w, b), zsend.at[w * 5 + s], zrecv.at[w * 4 + b],
+            place(w, b), place(w, b), zsend.at[min(w, 3) * 5 + s], zrecv.at[zslot(w, zwhich[s])],
             row=other if s in (1, 4) else near,
         )
 
     def own_copy(w, s):
         return remote(
-            source(w), place(w, row), zsend.at[w * 5 + s], zrecv.at[w * 4 + row],
+            source(w), place(w, row), zsend.at[min(w, 3) * 5 + s], zrecv.at[zslot(w, zwhich[s])],
             row=other if s == 1 else near,
         )
 
-    def z_wait(w, b):
-        z_copy(w, 0, b).wait_recv()
+    def z_wait(w, which):
+        z_copy(w, (0, 2, 3)[which], (near, other, far)[which]).wait_recv()
 
     def z_forward(w, s):
-        b = {2: other, 3: far, 4: near}[s]
-        z_wait(w, b)
-        z_copy(w, s, b).start()
+        which = {2: 1, 3: 2, 4: 0}[s]
+        z_wait(w, which)
+        z_copy(w, s, (near, other, far)[which]).start()
+
+    def z_sent(s):
+        for w in (0, 1, 2):
+            z_copy(w, s, row).wait_send()
+        both = f1.at[pl.ds(0, 2 * quarter)]
+        remote(both, both, zsend.at[15 + s], zrecv.at[0], row=near).wait_send()
 
     loads = [load(0, wq_in, wq), load(1, tok_in, tok)]
     for i, (src, dst) in enumerate(
@@ -442,7 +465,7 @@
         loads[i + 2].wait()
         vec[i : i + 1, : v.shape[0]] = v[...].astype(f32).reshape(1, -1)
     loads[1].wait()
-    pl.semaphore_wait(barrier, 10)
+    pl.semaphore_wait(barrier, 8 + row * (3 - row) // 2)
     for w in (0, 1, 2):
         own_copy(w, 0).start()
 
@@ -473,55 +496,55 @@
     lax.fori_loop(0, rows // chunk, norm1, 0)
 
     class Gather:
+        wait_on = (0, 1, 2, 2, 3, 3, 4, 4, 5, 5, 5, 5, 6, 6)
+
         def __init__(self, x, gi):
             self.x, self.gi = x, gi
 
         def copy(self, i, block, h, to):
             at = self.x.at[pl.ds(pl.multiple_of(block * rows + h * half, half), half)]
-            return remote(at, at, gsend.at[self.gi, i], grecv.at[self.gi, i], col=to)
-
-        def arrived(self, i, block, h):
-            self.copy(i, block, h, mate).wait_recv()
+            return remote(
+                at, at, gsend.at[self.gi], grecv.at[self.gi, self.wait_on[i]], col=to
+            )
+
+        def arrived(self, i, count):
+            at = self.x.at[pl.ds(0, count * half)]
+            remote(at, at, gsend.at[self.gi], grecv.at[self.gi, i], col=mate).wait_recv()
 
         def start(self):
             for i, h, to in ((0, 0, xn), (1, 1, yn), (2, 1, xn), (3, 0, yn), (6, 0, mate), (7, 1, mate)):
                 self.copy(i, me, h, to).start()
 
         def event0(self):
-            self.arrived(0, xn, 0)
+            self.arrived(0, 1)
             self.copy(4, xn, 0, yn).start()
             self.copy(8, xn, 0, mate).start()
-            self.arrived(1, yn, 1)
+            self.arrived(1, 1)
             self.copy(5, yn, 1, xn).start()
             self.copy(9, yn, 1, mate).start()
 
         def event1(self):
-            self.arrived(2, xn, 1)
+            self.arrived(2, 2)
             self.copy(10, xn, 1, mate).start()
-            self.arrived(3, yn, 0)
             self.copy(11, yn, 0, mate).start()
 
         def event2(self):
-            self.arrived(4, dn, 0)
+            self.arrived(3, 2)
             self.copy(12, dn, 0, mate).start()
-            self.arrived(5, dn, 1)
             self.copy(13, dn, 1, mate).start()
 
         def mate0(self):
-            self.arrived(6, mate, 0)
-            self.arrived(7, mate, 1)
+            self.arrived(4, 2)
 
         def mate1(self):
-            for i, block, h in ((8, xn, 0), (10, xn, 1), (9, yn, 1), (11, yn, 0)):
-                self.arrived(i, block + shift, h)
+            self.arrived(5, 4)
 
         def mate2(self):
-            for i, h in ((12, 0), (13, 1)):
-                self.arrived(i, dn + shift, h)
+            self.arrived(6, 2)
 
         def finish(self):
-            for i in range(14):
-                self.copy(i, me, 0, mate).wait_send()
+            at = self.x.at[pl.ds(0, 14 * half)]
+            remote(at, at, gsend.at[self.gi], grecv.at[self.gi, 0], col=mate).wait_send()
 
     first = Gather(x1, 0)
     first.start()
@@ -569,12 +592,13 @@
 
     @pl.when(end)
     def _():
-        q_wait(near)
+        q_wait(0)
 
     widen(near)
 
     @pl.when(middle)
     def _():
+        z_forward(2, 2)
         z_forward(2, 4)
         own_copy(3, 1).start()
         for w in (0, 1):
@@ -582,9 +606,15 @@
 
     first.event1()
 
+    p_on = (0, 1, 4, 2, 3, 4, 4, 4, 4)
+
     def pcopy(i, r, at, count, block, to):
         ref = pfull.at[pl.ds(at, count), lines(block, prows)]
-        return remote(ref, ref, psend.at[r, i], precv.at[r, i], col=to)
+        return remote(ref, ref, psend.at[r], precv.at[r, p_on[i]], col=to)
+
+    def punits(r, i, count):
+        ref = pfull.at[pl.ds(0, 2), pl.ds(0, count // 2 * prows)]
+        return remote(ref, ref, psend.at[r], precv.at[r, i], col=mate)
 
     def p_start(r, at):
         pcopy(0, r, at, 2, me, xn).start()
@@ -605,30 +635,23 @@
         pcopy(4, r, at + 1, 1, dn, xn).wait_recv()
         pcopy(8, r, at + 1, 1, dn, mate).start()
 
-    def p_mates(r, at):
-        pcopy(2, r, at, 2, mate, mate).wait_recv()
-        pcopy(5, r, at, 2, xn + shift, mate).wait_recv()
-        pcopy(6, r, at, 2, yn + shift, mate).wait_recv()
-        pcopy(7, r, at, 1, dn + shift, mate).wait_recv()
-        pcopy(8, r, at + 1, 1, dn + shift, mate).wait_recv()
-
-    def p_finish(r, at):
-        for i in (0, 1, 2, 5, 6):
-            pcopy(i, r, at, 2, me, mate).wait_send()
-        for i in (3, 4, 7, 8):
-            pcopy(i, r, at, 1, me, mate).wait_send()
+    def p_mates(r):
+        punits(r, 4, 8).wait_recv()
+
+    def p_finish(r):
+        punits(r, 0, 14).wait_send()
 
 
     @pl.when(end)
     def _():
-        z_wait(2, near)
+        z_wait(2, 0)
 
     p_start(0, lo)
 
     @pl.when(middle)
     def _():
-        z_forward(2, 2)
         z_forward(2, 3)
+        p_start(1, hi)
         own_copy(3, 0).start()
         z_forward(3, 4)
         own_copy(4, 1).start()
@@ -638,8 +661,8 @@
 
     @pl.when(end)
     def _():
-        q_wait(other)
-        q_wait(far)
+        q_wait(1)
+        q_wait(2)
 
     widen(other)
     widen(far)
@@ -649,20 +672,17 @@
     factor = 1.4426950408889634 / size**0.5
 
     def qkv_block(i, c):
-        @pl.when(i == 6)
+        @pl.when(jnp.logical_or(jnp.logical_and(i == 1, end), jnp.logical_and(i == 2, middle)))
         def _():
             p_forward(0, lo)
 
-        @pl.when(jnp.logical_and(i == 7, end))
-        def _():
-            z_wait(2, other)
-            z_wait(2, far)
-
-        @pl.when(i == 7)
-        def _():
+        @pl.when(jnp.logical_and(i == 2, end))
+        def _():
+            z_wait(2, 1)
+            z_wait(2, 2)
             p_start(1, hi)
 
-        at = lines(flipped(i))
+        at = lines(flipped(2 * i) // 2, 2 * rows)
         product = jnp.dot(x1[at, :], qwide[...], preferred_element_type=f32) + qrow[...]
         for g in range(groups):
             cols = slice(g * LANES, (g + 1) * LANES)
@@ -670,36 +690,35 @@
             qkv[at, cols] = (value * factor if g % 3 == 0 else value).astype(bf16)
         return c
 
-    lax.fori_loop(0, 8, qkv_block, 0)
+    lax.fori_loop(0, 4, qkv_block, 0)
 
     rest_lanes = prows - LANES
 
-    def a_copies(i, core, m, to):
+    def a_all(which):
+        ref = (heads_in, tails_in)[which].at[pl.ds(0, 7)]
+        return remote(ref, ref, asend.at[which], arecv.at[which], col=mate)
+
+    def a_copies(i, core, to):
         at = lines(core)
         tail = pl.ds(pl.multiple_of(core * half, half), half)
         return (
             remote(
-                heads_out.at[i, at], heads_in.at[me], asend.at[0, m], arecv.at[0, m], col=to
+                heads_out.at[i, at], heads_in.at[me], asend.at[0], arecv.at[0], col=to
             ),
             remote(
-                tails_out.at[i, tail], tails_in.at[me], asend.at[1, m], arecv.at[1, m], col=to
+                tails_out.at[i, tail], tails_in.at[me], asend.at[1], arecv.at[1], col=to
             ),
         )
 
     def attend_block(i, c):
-        @pl.when(i == 1)
+        @pl.when(jnp.logical_and(i == 1, middle))
+        def _():
+            z_forward(3, 2)
+            z_forward(4, 4)
+
+        @pl.when(i == 2)
         def _():
             p_last(0, lo)
-
-        @pl.when(jnp.logical_and(i == 1, middle))
-        def _():
-            z_forward(3, 2)
-            z_wait(4, near)
-            for w in (5, 6):
-                z_copy(w, 4, near).start()
-
-        @pl.when(i == 3)
-        def _():
             p_forward(1, hi)
 
         chip = flipped(6 - 2 * i) // 2
@@ -739,7 +758,7 @@
 
             @pl.when(to != me)
             def _():
-                for c in a_copies(i, core, 6 - 2 * i + (core + me) % 2, to):
+                for c in a_copies(i, core, to):
                     c.start()
 
         return c
@@ -754,18 +773,10 @@
     first.finish()
     heads_in[me] = heads_out[3, lines(me % 2), :]
     tails_in[me] = tails_out[3, lines(me % 2, half), :]
-    p_mates(0, lo)
-    p_mates(1, hi)
-    for m in range(1, 8):
-        for ref, out, n, which in (
-            (heads_in, heads_out, rows, 0), (tails_in, tails_out, half, 1)
-        ):
-            arrived = remote(
-                out.at[0, pl.ds(0, n)], ref.at[flipped(m)], asend.at[which, m],
-                arecv.at[which, m], col=mate,
-            )
-            arrived.wait_recv()
-
+    p_mates(0)
+    p_mates(1)
+    a_all(0).wait_recv()
+    a_all(1).wait_recv()
     for d in range(8):
         base = d * prows
         ctx[:, base : base + LANES] = heads_in[d]
@@ -794,9 +805,9 @@
 
     @pl.when(end)
     def _():
-        z_wait(3, near)
-        z_wait(3, other)
-        z_wait(3, far)
+        z_wait(3, 0)
+        z_wait(3, 1)
+        z_wait(3, 2)
 
     starts, done = [], 0
     for width in pieces:
@@ -810,28 +821,28 @@
             self.cols = pl.ds(pl.multiple_of(starts[p], LANES), pieces[p])
 
         def copy(self, i, src, dst, to):
-            return remote(src, dst, ssend.at[self.p, i], srecv.at[self.p, i], col=to)
+            return remote(
+                src, dst, ssend.at[self.p, min(i // 4, 1)], srecv.at[self.p, min(i, 6)], col=to
+            )
 
         def of(self, ref, k, h):
             return ref.at[k, pl.ds(h * half, half), self.cols]
 
         def to_mate(self, k):
             block = flipped(6 - 2 * k + 1)
-            return self.copy(k, part.at[lines(block), self.cols], mated.at[k, :, self.cols], mate)
-
-        def compute(self, stage):
-            weight = f2.at[self.cols]
-
-            def body(t, c):
-                k = 2 - t % 2 if stage == 0 else 3 * (t % 2)
-                block = flipped(6 - 2 * k + 1 - t // 2)
-                at = lines(block)
-                part[at, self.cols] = project_back(hid[at, :], weight[...]).astype(bf16)
-
-                @pl.when(t < 2)
-                def _():
-                    self.to_mate(k).start()
-
+            return remote(
+                part.at[lines(block), self.cols], mated.at[k, :, self.cols],
+                ssend.at[self.p, 0], srecv.at[self.p, k], col=mate,
+            )
+
+        def compute(self, k):
+            at = lines(flipped(6 - 2 * k) // 2, 2 * rows)
+            part[at, self.cols] = project_back(hid[at, :], f2[self.cols, :]).astype(bf16)
+            self.to_mate(k).start()
+
+        def compute_all(self):
+            def body(k, c):
+                self.compute(k)
                 return c
 
             lax.fori_loop(0, 4, body, 0)
@@ -859,13 +870,11 @@
             }[i]
             return self.copy(i, self.of(sums, k, h), dst, to)
 
-        def open_direct(self):
-            self.to_mate(2).wait_recv()
-            self.put(2, 0, self.mine(2, 0))
-            self.c(6).start()
-            self.to_mate(1).wait_recv()
-            self.put(1, 1, self.mine(1, 1))
-            self.c(7).start()
+        def direct(self, k):
+            h = {1: 1, 2: 0}[k]
+            self.to_mate(k).wait_recv()
+            self.put(k, h, self.mine(k, h))
+            self.c({1: 7, 2: 6}[k]).start()
 
         def open_relayed(self):
             self.to_mate(0).wait_recv()
@@ -884,8 +893,8 @@
 
         def close(self):
             self.to_mate(3).wait_recv()
-            for i in (6, 7, 8, 9):
-                self.c(i).wait_recv()
+            ref = landed.at[:, :, self.cols]
+            self.copy(6, ref, ref, mate).wait_recv()
             for h in (0, 1):
                 at = slice(h * half, (h + 1) * half)
                 total = (
@@ -893,48 +902,58 @@
                     + landed[0, at, self.cols].astype(f32)
                     + landed[1, at, self.cols].astype(f32)
                 )
-                value = resid[at, self.cols] + total + vec[5:6, self.cols]
-                o_ref[at, self.cols] = value.astype(o_ref.dtype)
+                resid[at, self.cols] = resid[at, self.cols] + total + vec[5:6, self.cols]
+            self.out().start()
+
+        def out(self):
+            return pltpu.make_async_copy(
+                resid.at[:, self.cols], o_ref.at[:, self.cols], osem.at[self.p]
+            )
 
         def finish(self):
-            for k in range(4):
-                self.to_mate(k).wait_send()
-            for i in range(4, 10):
-                self.c(i).wait_send()
-
-    one, two, three, four = (Piece(p) for p in range(4))
+            self.out().wait()
+            ref = mated.at[:, :, self.cols]
+            self.copy(0, ref, ref, mate).wait_send()
+            ref = sums.at[:, :, self.cols]
+            self.copy(6, ref, ref, mate).wait_send()
+
+    one, two, after, three, four = (Piece(p) for p in range(5))
 
     def fc1_block(i, c):
+        @pl.when(i == 0)
+        def _():
+            second.mate0()
+
         @pl.when(i == 1)
         def _():
-            second.mate0()
-
-        @pl.when(i == 2)
-        def _():
             second.event1()
 
+        @pl.when(jnp.logical_and(i == 1, middle))
+        def _():
+            z_wait(4, 1)
+            z_copy(7, 2, other).start()
+            z_copy(8, 2, other).start()
+
+        @pl.when(i == 1)
+        def _():
+            second.mate1()
+
         @pl.when(i == 3)
         def _():
-            second.mate1()
-
-        @pl.when(i == 6)
-        def _():
             second.event2()
 
-        @pl.when(jnp.logical_and(i == 2, middle))
-        def _():
-            z_forward(4, 2)
-
-        @pl.when(jnp.logical_and(i == 5, middle))
-        def _():
-            z_forward(5, 3)
-            z_forward(6, 3)
-
-        @pl.when(i == 7)
-        def _():
+        @pl.when(jnp.logical_and(i == 3, middle))
+        def _():
+            z_wait(4, 2)
+            z_copy(5, 3, far).start()
+            z_copy(6, 3, far).start()
+
+        @pl.when(i == 3)
+        def _():
+            one.direct(1)
             second.mate2()
 
-        at = lines(flipped(i))
+        at = lines(flipped(2 * i) // 2, 2 * rows)
         for c0 in range(0, hidden, 2 * LANES):
             cols = slice(c0, c0 + 2 * LANES)
             value = jnp.dot(x2[at, :], f1[:, cols], preferred_element_type=f32) + vec[7:8, cols]
@@ -942,76 +961,81 @@
                 0.5 * value * (1.0 + lax.erf(value * 0.7071067811865476))
             ).astype(bf16)
 
-        @pl.when(jnp.logical_and(i == 5, end))
-        def _():
-            z_wait(4, near)
-
-        @pl.when(i == 5)
-        def _():
-            one.compute(0)
-            one.open_direct()
+        @pl.when(jnp.logical_and(i == 1, end))
+        def _():
+            z_wait(4, 0)
+
+        @pl.when(i == 2)
+        def _():
+            one.direct(2)
+
+        @pl.when(i > 0)
+        def _():
+            one.compute(3 - i)
 
         return c
 
-    lax.fori_loop(0, 8, fc1_block, 0)
-
-    one.compute(1)
+    lax.fori_loop(0, 4, fc1_block, 0)
+
+    def open_all(piece):
+        piece.open_relayed()
+        piece.direct(2)
+        piece.direct(1)
+
+    one.compute(3)
     one.open_relayed()
 
     @pl.when(end)
     def _():
-        z_wait(4, other)
-
-    two.compute(0)
-    two.open_direct()
-    two.compute(1)
-    two.open_relayed()
+        z_wait(7, 1)
+
+    two.compute_all()
+    open_all(two)
     one.pass_on()
 
     @pl.when(end)
     def _():
-        z_wait(5, far)
-
-    three.compute(0)
-    three.open_direct()
-    three.compute(1)
-    three.open_relayed()
+        z_wait(8, 1)
+
+    after.compute_all()
+    open_all(after)
     two.pass_on()
+
+    @pl.when(end)
+    def _():
+        z_wait(5, 2)
+
+    three.compute_all()
+    open_all(three)
+    after.pass_on()
+
+    @pl.when(end)
+    def _():
+        z_wait(6, 2)
+
+    four.compute_all()
+    open_all(four)
+    three.pass_on()
     one.close()
-
-    @pl.when(end)
-    def _():
-        z_wait(6, far)
-
-    four.compute(0)
-    four.open_direct()
-    four.compute(1)
-    four.open_relayed()
-    three.pass_on()
+    four.pass_on()
     two.close()
-    four.pass_on()
+    after.close()
     three.close()
     four.close()
 
-    for piece in (one, two, three, four):
+    for piece in (one, two, after, three, four):
         piece.finish()
     second.finish()
-    p_finish(0, lo)
-    p_finish(1, hi)
-    for m in range(1, 8):
-        for c in a_copies(0, 0, m, mate):
-            c.wait_send()
-    for w in range(5):
-        own_copy(w, 0).wait_send()
+    p_finish(0)
+    p_finish(1)
+    a_all(0).wait_send()
+    a_all(1).wait_send()
+    z_sent(0)
 
     @pl.when(middle)
     def _():
-        for w in range(5):
-            own_copy(w, 1).wait_send()
-            z_copy(w, 2, other).wait_send()
-        for w in (0, 1, 2, 3, 5, 6):
-            z_copy(w, 3, far).wait_send()
-            z_copy(w, 4, near).wait_send()
+        for way in range(1, 5):
+            z_sent(way)
 
 
 def layer_call(plan, *arrays):
@@ -1025,7 +1049,7 @@
         functools.partial(layer_kernel, plan),
         out_shape=jax.ShapeDtypeStruct((rows, features), f32),
         in_specs=[pl.BlockSpec(memory_space=pl.ANY)] * 13,
-        out_specs=pl.BlockSpec(memory_space=pltpu.VMEM),
+        out_specs=pl.BlockSpec(memory_space=pl.ANY),
         scratch_shapes=[
             pltpu.VMEM((rows, features), bf16),
             pltpu.VMEM(arrays[9].shape, bf16),
@@ -1051,12 +1075,12 @@
             pltpu.VMEM((3, rows, features), bf16),
             pltpu.VMEM((2, rows // 2, features), bf16),
             pltpu.VMEM((2, rows, features), bf16),
-            dma((13,)),
-            dma((35,)), dma((28,)),
-            dma((2, 14)), dma((2, 14)),
-            dma((2, 9)), dma((2, 9)),
-            dma((2, 8)), dma((2, 8)),
-            dma((4, 10)), dma((4, 10)),
+            dma((13,)), dma((5,)),
+            dma((20,)), dma((19,)),
+            dma((2,)), dma((2, 7)),
+            dma((2,)), dma((2, 5)),
+            dma((2,)), dma((2,)),
+            dma((5, 2)), dma((5, 7)),
         ],
         compiler_params=pltpu.CompilerParams(
             collective_id=3, has_side_effects=True, vmem_limit_bytes=60 * 1024 * 1024

time: 128 us -> 123 us (0.961)
  Pallas kernels: 126 us -> 120 us
    pallas_call x1, Pallas kernels: 126 us -> 120 us  [layer_call(): pl.pallas_call(functools.partial(layer_kernel, plan), out_shape=jax.Shape...]
where the time goes in v2:
time: 123 us
  Pallas kernels  120 us (98%)
  other arithmetic  2.3 us (2%)
    pallas_call x1, Pallas kernels, layer_call(): pl.pallas_call(functools.partial(layer_kernel, plan), out_shape=jax.Shape...  120 us

profile of v2, /device:TPU:0, one launch (start us, length us, event | category | flops | bytes accessed | tf_op | source)
XLA Modules:
  0.0 122.6 jit_solution(6836374842868108511)
XLA Ops:
  0.0 120.3 %layer.1 = f32[256,1408]{1,0:T(8,128)} custom-call(bf16[256,1408]{1,0:T(8,128)(2,1)} %tok_in.1, bf16[1408]{0:T(1024)(128)(2,1)} %g1.1, bf16[1408]{0:T(1024)(128)(2,1)} %c1.1, bf16[528]{0:T(1024)(128)(2,1)} %qb.1, bf16[1408]{0:T(1024)(128)(2,1)} %pb.1, bf16[1408]{0:T(1024)(128)(2,1)} %g2.1, bf16[1408]{0:T(1024)(128)(2,1)} %c2.1, bf16[768]{0:T(1024)(128)(2,1)} %d1.1, ...), custom_call_target="tpu_custom_call" | custom-call | tf_op jit(solution)/shard_map/layer/pallas_call | solution.py:1048
  120.3 2.3 %convert_element_type.3 = bf16[256,1408]{1,0:T(8,128)(2,1)} convert(f32[256,1408]{1,0:T(8,128)} %layer.1) | non-fusion elementwise | flops 360448 | bytes 2162688 | tf_op jit(solution)/shard_map/convert_element_type | solution.py:1119

commit v3 on v2

--- a/solution.py
+++ b/solution.py
@@ -332,7 +332,7 @@
     tok, wq, v1, v2, v3, v4, v5, v6, v7, v8,
     vec, x1, x2, qmain, qrest, qwide, qrow, qkv, ctx, heads_out, tails_out, heads_in, tails_in, pfull, f1, f2, resid,
     mated, sums, relay, landed,
-    lsem, osem, zsend, zrecv, gsend, grecv, psend, precv, asend, arecv, ssend, srecv,
+    lsem, zsend, zrecv, gsend, grecv, psend, precv, asend, arecv, ssend, srecv,
 ):
     heads, size, rows = plan["heads"], plan["size"], plan["rows"]
     features, quarter = plan["features"], plan["quarter"]
@@ -902,16 +902,9 @@
                     + landed[0, at, self.cols].astype(f32)
                     + landed[1, at, self.cols].astype(f32)
                 )
-                resid[at, self.cols] = resid[at, self.cols] + total + vec[5:6, self.cols]
-            self.out().start()
-
-        def out(self):
-            return pltpu.make_async_copy(
-                resid.at[:, self.cols], o_ref.at[:, self.cols], osem.at[self.p]
-            )
+                o_ref[at, self.cols] = resid[at, self.cols] + total + vec[5:6, self.cols]
 
         def finish(self):
-            self.out().wait()
             ref = mated.at[:, :, self.cols]
             self.copy(0, ref, ref, mate).wait_send()
             ref = sums.at[:, :, self.cols]
@@ -1047,9 +1040,9 @@
     dma = pltpu.SemaphoreType.DMA
     return pl.pallas_call(
         functools.partial(layer_kernel, plan),
-        out_shape=jax.ShapeDtypeStruct((rows, features), f32),
+        out_shape=pltpu.VMEM((rows, features), f32),
         in_specs=[pl.BlockSpec(memory_space=pl.ANY)] * 13,
-        out_specs=pl.BlockSpec(memory_space=pl.ANY),
+        out_specs=pl.BlockSpec(memory_space=pltpu.VMEM),
         scratch_shapes=[
             pltpu.VMEM((rows, features), bf16),
             pltpu.VMEM(arrays[9].shape, bf16),
@@ -1075,7 +1068,7 @@
             pltpu.VMEM((3, rows, features), bf16),
             pltpu.VMEM((2, rows // 2, features), bf16),
             pltpu.VMEM((2, rows, features), bf16),
-            dma((13,)), dma((5,)),
+            dma((13,)),
             dma((20,)), dma((19,)),
             dma((2,)), dma((2, 7)),
             dma((2,)), dma((2, 5)),

time: 123 us -> 121 us (0.984)
  other arithmetic: 2.3 us -> 0.93 us
    convert_element_type x1, other arithmetic: 2.3 us -> 0.93 us  [local(): return layer_call(plan, tokens_in, ln1_gain, ln1_bias, qkv_bias, proj_bia...]
where the time goes in v3:
time: 121 us
  Pallas kernels  120 us (99%)
    pallas_call x1, Pallas kernels, layer_call(): pl.pallas_call(functools.partial(layer_kernel, plan), out_shape=pltpu.VME...  120 us

profile of v3, /device:TPU:0, one launch (start us, length us, event | category | flops | bytes accessed | tf_op | source)
XLA Modules:
  0.0 120.5 jit_solution(13893426784778159255)
XLA Ops:
  0.0 119.6 %layer.1 = f32[256,1408]{1,0:T(8,128)S(1)} custom-call(bf16[256,1408]{1,0:T(8,128)(2,1)} %tok_in.1, bf16[1408]{0:T(1024)(128)(2,1)} %g1.1, bf16[1408]{0:T(1024)(128)(2,1)} %c1.1, bf16[528]{0:T(1024)(128)(2,1)} %qb.1, bf16[1408]{0:T(1024)(128)(2,1)} %pb.1, bf16[1408]{0:T(1024)(128)(2,1)} %g2.1, bf16[1408]{0:T(1024)(128)(2,1)} %c2.1, bf16[768]{0:T(1024)(128)(2,1)} %d1.1, ...), custom_call_target="tpu_custom_call" | custom-call | tf_op jit(solution)/shard_map/layer/pallas_call | solution.py:1041
  119.6 0.9 convert_element_type.3

commit v4 on v3

--- a/solution.py
+++ b/solution.py
@@ -305,7 +305,7 @@
     whole = qkv_width // LANES * LANES
     rest = qkv_width - whole
     ok = (
-        hidden == 3 * heads * LANES and own_rows % 32 == 0 and features % LANES == 0 and quarter % 32 == 0
+        hidden == 3 * heads * LANES and own_rows % 128 == 0 and features % LANES == 0 and quarter % 32 == 0
         and hidden % LANES == 0 and 0 < rest and proj_rows == heads * size
         and proj_rows % 16 == 0 and 0 < proj_rows - LANES <= LANES // 2
         and 8 * proj_rows == features and size < LANES and whole // size == 3 * heads - 1
@@ -360,7 +360,7 @@
         return bits[0] + 2 * bits[1] + 4 * bits[2]
 
     barrier = pltpu.get_barrier_semaphore()
-    for step in range(1, 8):
+    for step in range(1, 6):
         pl.semaphore_signal(
             barrier, inc=1, device_id={"col": flipped(step)}, device_id_type=MESH
         )
@@ -461,23 +461,24 @@
     qmain[lines(row, quarter), :] = turned[:, :whole]
     for j in range(quarter // 32):
         qrest[row, :, j * rest : (j + 1) * rest] = turned[32 * j : 32 * (j + 1), whole:]
+    pl.semaphore_wait(barrier, 6 + row * (3 - row) // 2)
+    for w in (0, 1, 2):
+        own_copy(w, 0).start()
+
+    @pl.when(middle)
+    def _():
+        for w in (0, 1, 2):
+            own_copy(w, 1).start()
+
+    @pl.when(end)
+    def _():
+        for w in (3, 4):
+            own_copy(w, 0).start()
+
     for i, v in enumerate((v1, v2, v3, v4, v5, v6, v7, v8)):
         loads[i + 2].wait()
         vec[i : i + 1, : v.shape[0]] = v[...].astype(f32).reshape(1, -1)
     loads[1].wait()
-    pl.semaphore_wait(barrier, 8 + row * (3 - row) // 2)
-    for w in (0, 1, 2):
-        own_copy(w, 0).start()
-
-    @pl.when(middle)
-    def _():
-        for w in (0, 1, 2):
-            own_copy(w, 1).start()
-
-    @pl.when(end)
-    def _():
-        for w in (3, 4):
-            own_copy(w, 0).start()
 
     def norm(values, g, b):
         mean = jnp.mean(values, axis=-1, keepdims=True)
@@ -487,13 +488,21 @@
 
     chunk = 32
 
-    def norm1(i, c):
+    def norm1(i):
         at = pl.ds(pl.multiple_of(i * chunk, chunk), chunk)
         to = pl.ds(pl.multiple_of(me * rows + i * chunk, chunk), chunk)
         x1[to, :] = norm(tok[at, :].astype(f32), 0, 1).astype(bf16)
-        return c
-
-    lax.fori_loop(0, rows // chunk, norm1, 0)
+
+    some = half // chunk // 2
+
+    def two_steps(body, gather):
+        for part in (0, 1):
+            def step(t, c):
+                body(t % some + t // some * 2 * some + part * some)
+                return c
+
+            lax.fori_loop(0, 2 * some, step, 0)
+            gather.start(part)
 
     class Gather:
         wait_on = (0, 1, 2, 2, 3, 3, 4, 4, 5, 5, 5, 5, 6, 6)
@@ -511,9 +520,15 @@
             at = self.x.at[pl.ds(0, count * half)]
             remote(at, at, gsend.at[self.gi], grecv.at[self.gi, i], col=mate).wait_recv()
 
-        def start(self):
-            for i, h, to in ((0, 0, xn), (1, 1, yn), (2, 1, xn), (3, 0, yn), (6, 0, mate), (7, 1, mate)):
-                self.copy(i, me, h, to).start()
+        def start(self, part):
+            for i, to in ((0, xn), (1, yn)):
+                at = self.x.at[
+                    pl.ds(pl.multiple_of(me * rows + i * half + part * half // 2, half // 2), half // 2)
+                ]
+                remote(at, at, gsend.at[self.gi], grecv.at[self.gi, i], col=to).start()
+            if part:
+                for i, h, to in ((2, 1, xn), (3, 0, yn), (6, 0, mate), (7, 1, mate)):
+                    self.copy(i, me, h, to).start()
 
         def event0(self):
             self.arrived(0, 1)
@@ -547,7 +562,7 @@
             remote(at, at, gsend.at[self.gi], grecv.at[self.gi, 0], col=mate).wait_send()
 
     first = Gather(x1, 0)
-    first.start()
+    two_steps(norm1, first)
     qrow[...] = jnp.zeros_like(qrow)
     for g in range(groups):
         qrow[:, g * LANES : g * LANES + size] = vec[6:7, g * size : (g + 1) * size]
@@ -790,17 +805,15 @@
             ctx[...], pfull[b], preferred_element_type=f32
         )
 
-    def norm2(i, c):
+    def norm2(i):
         at = pl.ds(pl.multiple_of(i * chunk, chunk), chunk)
         to = pl.ds(pl.multiple_of(me * rows + i * chunk, chunk), chunk)
         value = tok[at, :].astype(f32) + resid[at, :] + vec[4:5, :]
         resid[at, :] = value
         x2[to, :] = norm(value, 2, 3).astype(bf16)
-        return c
-
-    lax.fori_loop(0, rows // chunk, norm2, 0)
+
     second = Gather(x2, 1)
-    second.start()
+    two_steps(norm2, second)
     second.event0()
 
     @pl.when(end)
@@ -902,7 +915,8 @@
                     + landed[0, at, self.cols].astype(f32)
                     + landed[1, at, self.cols].astype(f32)
                 )
-                o_ref[at, self.cols] = resid[at, self.cols] + total + vec[5:6, self.cols]
+                value = resid[at, self.cols] + total + vec[5:6, self.cols]
+                o_ref[at, self.cols] = value.astype(bf16)
 
         def finish(self):
             ref = mated.at[:, :, self.cols]
@@ -1040,7 +1054,7 @@
     dma = pltpu.SemaphoreType.DMA
     return pl.pallas_call(
         functools.partial(layer_kernel, plan),
-        out_shape=pltpu.VMEM((rows, features), f32),
+        out_shape=pltpu.VMEM((rows, features), bf16),
         in_specs=[pl.BlockSpec(memory_space=pl.ANY)] * 13,
         out_specs=pl.BlockSpec(memory_space=pltpu.VMEM),
         scratch_shapes=[
@@ -1109,7 +1123,7 @@
         return layer_call(
             plan, tokens_in, ln1_gain, ln1_bias, qkv_bias, proj_bias, ln2_gain, ln2_bias, fc1_bias,
             fc2_bias, qkv_weight.T, proj_weight, fc1_weight, fc2_weight,
-        ).astype(jnp.bfloat16)
+        )
     inputs = tokens_in.astype(jnp.float32)
     qkv_full = gather_row(qkv_weight, 0)
     proj_full = gather_row(proj_weight, 1)

time: 121 us -> 120 us (level)
  no operation moved by 1% of the time
where the time goes in v4:
time: 120 us
  Pallas kernels  119 us (99%)
    pallas_call x1, Pallas kernels, layer_call(): pl.pallas_call(functools.partial(layer_kernel, plan), out_shape=pltpu.VME...  119 us

profile of v4, /device:TPU:0, one launch (start us, length us, event | category | flops | bytes accessed | tf_op | source)
XLA Modules:
  0.0 120.3 jit_solution(8456839429305563535)
XLA Ops:
  0.0 119.4 %layer.1 = bf16[256,1408]{1,0:T(8,128)(2,1)S(1)} custom-call(bf16[256,1408]{1,0:T(8,128)(2,1)} %tok_in.1, bf16[1408]{0:T(1024)(128)(2,1)} %g1.1, bf16[1408]{0:T(1024)(128)(2,1)} %c1.1, bf16[528]{0:T(1024)(128)(2,1)} %qb.1, bf16[1408]{0:T(1024)(128)(2,1)} %pb.1, bf16[1408]{0:T(1024)(128)(2,1)} %g2.1, bf16[1408]{0:T(1024)(128)(2,1)} %c2.1, bf16[768]{0:T(1024)(128)(2,1)} %d1.1, ...), custom_call_target="tpu_custom_call" | custom-call | tf_op jit(solution)/shard_map/layer/pallas_call | solution.py:1055
  119.4 0.9 copy.15

commit v5 on v4

--- a/solution.py
+++ b/solution.py
@@ -998,7 +998,6 @@
 
     two.compute_all()
     open_all(two)
-    one.pass_on()
 
     @pl.when(end)
     def _():
@@ -1006,22 +1005,27 @@
 
     after.compute_all()
     open_all(after)
+    one.pass_on()
+
+    @pl.when(end)
+    def _():
+        z_wait(5, 2)
+
+    three.compute_all()
+    three.open_relayed()
     two.pass_on()
+    after.pass_on()
 
     @pl.when(end)
     def _():
-        z_wait(5, 2)
-
-    three.compute_all()
-    open_all(three)
-    after.pass_on()
-
-    @pl.when(end)
-    def _():
         z_wait(6, 2)
 
     four.compute_all()
-    open_all(four)
+    four.open_relayed()
+    for piece in (three, four):
+        piece.direct(2)
+        piece.direct(1)
+
     three.pass_on()
     one.close()
     four.pass_on()

time: 120 us -> 119 us (level)
  no operation moved by 1% of the time
where the time goes in v5:
time: 119 us
  Pallas kernels  118 us (99%)
    pallas_call x1, Pallas kernels, layer_call(): pl.pallas_call(functools.partial(layer_kernel, plan), out_shape=pltpu.VME...  118 us

profile of v5, /device:TPU:0, one launch (start us, length us, event | category | flops | bytes accessed | tf_op | source)
XLA Modules:
  0.0 119.1 jit_solution(2441227610723895382)
XLA Ops:
  0.0 118.2 %layer.1 = bf16[256,1408]{1,0:T(8,128)(2,1)S(1)} custom-call(bf16[256,1408]{1,0:T(8,128)(2,1)} %tok_in.1, bf16[1408]{0:T(1024)(128)(2,1)} %g1.1, bf16[1408]{0:T(1024)(128)(2,1)} %c1.1, bf16[528]{0:T(1024)(128)(2,1)} %qb.1, bf16[1408]{0:T(1024)(128)(2,1)} %pb.1, bf16[1408]{0:T(1024)(128)(2,1)} %g2.1, bf16[1408]{0:T(1024)(128)(2,1)} %c2.1, bf16[768]{0:T(1024)(128)(2,1)} %d1.1, ...), custom_call_target="tpu_custom_call" | custom-call | tf_op jit(solution)/shard_map/layer/pallas_call | solution.py:1059
  118.2 0.9 copy.15

commit v6 on v5

--- a/solution.py
+++ b/solution.py
@@ -926,47 +926,52 @@
 
     one, two, after, three, four = (Piece(p) for p in range(5))
 
-    def fc1_block(i, c):
-        @pl.when(i == 0)
-        def _():
-            second.mate0()
-
-        @pl.when(i == 1)
-        def _():
-            second.event1()
-
-        @pl.when(jnp.logical_and(i == 1, middle))
-        def _():
-            z_wait(4, 1)
-            z_copy(7, 2, other).start()
-            z_copy(8, 2, other).start()
-
-        @pl.when(i == 1)
-        def _():
-            second.mate1()
-
-        @pl.when(i == 3)
-        def _():
-            second.event2()
-
-        @pl.when(jnp.logical_and(i == 3, middle))
-        def _():
-            z_wait(4, 2)
-            z_copy(5, 3, far).start()
-            z_copy(6, 3, far).start()
-
-        @pl.when(i == 3)
-        def _():
-            one.direct(1)
-            second.mate2()
-
-        at = lines(flipped(2 * i) // 2, 2 * rows)
+    def fc1_rows(block):
+        at = lines(block)
         for c0 in range(0, hidden, 2 * LANES):
             cols = slice(c0, c0 + 2 * LANES)
             value = jnp.dot(x2[at, :], f1[:, cols], preferred_element_type=f32) + vec[7:8, cols]
             hid[at, cols] = (
                 0.5 * value * (1.0 + lax.erf(value * 0.7071067811865476))
             ).astype(bf16)
+
+    def fc1_block(i, c):
+        @pl.when(i == 1)
+        def _():
+            second.event1()
+
+        @pl.when(jnp.logical_and(i == 1, middle))
+        def _():
+            z_wait(4, 1)
+            z_copy(7, 2, other).start()
+            z_copy(8, 2, other).start()
+
+        @pl.when(i == 3)
+        def _():
+            second.event2()
+
+        @pl.when(jnp.logical_and(i == 3, middle))
+        def _():
+            z_wait(4, 2)
+            z_copy(5, 3, far).start()
+            z_copy(6, 3, far).start()
+
+        fc1_rows(flipped(2 * i))
+
+        @pl.when(i == 0)
+        def _():
+            second.mate0()
+
+        @pl.when(i == 1)
+        def _():
+            second.mate1()
+
+        @pl.when(i == 3)
+        def _():
+            one.direct(1)
+            second.mate2()
+
+        fc1_rows(flipped(2 * i + 1))
 
         @pl.when(jnp.logical_and(i == 1, end))
         def _():

time: 119 us -> 119 us (level)
  no operation moved by 1% of the time
where the time goes in v6:
time: 119 us
  Pallas kernels  118 us (99%)
    pallas_call x1, Pallas kernels, layer_call(): pl.pallas_call(functools.partial(layer_kernel, plan), out_shape=pltpu.VME...  118 us

profile of v6, /device:TPU:0, one launch (start us, length us, event | category | flops | bytes accessed | tf_op | source)
XLA Modules:
  0.0 119.1 jit_solution(18410351868709945763)
XLA Ops:
  0.0 118.2 %layer.1 = bf16[256,1408]{1,0:T(8,128)(2,1)S(1)} custom-call(bf16[256,1408]{1,0:T(8,128)(2,1)} %tok_in.1, bf16[1408]{0:T(1024)(128)(2,1)} %g1.1, bf16[1408]{0:T(1024)(128)(2,1)} %c1.1, bf16[528]{0:T(1024)(128)(2,1)} %qb.1, bf16[1408]{0:T(1024)(128)(2,1)} %pb.1, bf16[1408]{0:T(1024)(128)(2,1)} %g2.1, bf16[1408]{0:T(1024)(128)(2,1)} %c2.1, bf16[768]{0:T(1024)(128)(2,1)} %d1.1, ...), custom_call_target="tpu_custom_call" | custom-call | tf_op jit(solution)/shard_map/layer/pallas_call | solution.py:1064
  118.2 0.9 copy.15
